TPU v7x, 8 devices: a whole 2x2x1 slice. The times are simulated.
8 devices in a mesh: dp: 1 (over z), ep: 8 (over y, x, core).
Axes of the slice: x: 2, y: 2, z: 1, core: 2. Of those that a mesh axis runs over, the one named last changes fastest.
Arguments:
- tokens: bfloat16 [2048, 2048], P(('dp', 'ep'))
- logits: float32 [2048, 256], P(('dp', 'ep'))
- w_in: bfloat16 [256, 2048, 512], P('ep')
- w_out: bfloat16 [256, 512, 2048], P('ep')
Outputs:
- output: bfloat16 [2048, 2048], P(('dp', 'ep'))
All inputs are finite; a program needn't handle non-finite values.
Results may differ from a plain program's by a relative error of at most 0.001.
Values are sent between devices in bfloat16 or wider.
A program may use at most 1 GiB of HBM per device.

v0:
```python
import jax
import jax.numpy as jnp
from jax import lax
from jax.sharding import PartitionSpec as P

CAP_FACTOR = 2


def solution(mesh):
    group = mesh.shape["ep"]
    row_spec = P(("dp", "ep"), None)
    expert_spec = P("ep", None, None)

    def device_step(tok_loc, logit_loc, w_in, w_out):
        tok_dev, d_model = tok_loc.shape
        experts = logit_loc.shape[1]
        exp_dev = w_in.shape[0]
        capacity = tok_dev * group * CAP_FACTOR // experts
        half_cap = capacity // 2
        gates = jax.nn.softmax(logit_loc, axis=-1)
        cand_score, cand_idx = lax.top_k(logit_loc.T, half_cap)
        cand_gate = jnp.take_along_axis(gates.T, cand_idx, axis=1)
        cand_rows = tok_loc[cand_idx]
        recv_score = lax.all_to_all(cand_score, "ep", 0, 1, tiled=True)
        recv_rows = lax.all_to_all(cand_rows, "ep", 0, 1, tiled=True)
        sel_pos = lax.top_k(recv_score, capacity)[1]
        picked = jnp.take_along_axis(recv_rows, sel_pos[:, :, None], axis=1)
        hidden = jax.nn.gelu(jnp.einsum("ecd,edf->ecf", picked, w_in, preferred_element_type=jnp.float32), approximate=False).astype(jnp.bfloat16)
        expert_out = jnp.einsum("ecf,efd->ecd", hidden, w_out, preferred_element_type=jnp.float32).astype(jnp.bfloat16)
        slot_out = jnp.zeros_like(recv_rows).at[jnp.arange(exp_dev)[:, None], sel_pos].set(expert_out)
        back_out = lax.all_to_all(slot_out, "ep", 1, 0, tiled=True)
        weighted = cand_gate[:, :, None] * back_out.astype(jnp.float32)
        combined = jax.ops.segment_sum(weighted.reshape(-1, d_model), cand_idx.reshape(-1), num_segments=tok_dev)
        return (tok_loc.astype(jnp.float32) + combined).astype(jnp.bfloat16)

    return jax.shard_map(device_step, mesh=mesh, in_specs=(row_spec, row_spec, expert_spec, expert_spec), out_specs=row_spec, check_vma=False)
```

profile of v0, /device:TPU:0, one launch (start us, length us, event | category | flops | bytes accessed | tf_op | source)
XLA Modules:
  0.0 449.5 jit_solution(2183144403503322728)
XLA Ops:
  0.0 0.0 copy-start
  0.0 6.9 %top_k.18 = (f32[256,256]{0,1:T(8,128)S(1)}, s32[256,256]{0,1:T(8,128)S(1)}) sort(f32[256,256]{0,1:T(8,128)} %bitcast.51, s32[256,256]{0,1:T(8,128)S(1)} %top_k.17.clone), dimensions={1}, to_apply=%region_0.0 | sort | flops 1048576 | bytes 1048576 | tf_op jit(solution)/shard_map/top_k | solution.py:21
  6.9 0.1 copy.38
  7.1 0.1 copy.28
  7.1 0.7 reshape.79
  7.8 4.3 all-to-all-start
  12.1 0.1 copy.39
  12.3 0.0 copy-start.2
  12.3 0.7 copy-done.2
  13.0 0.1 reshape.39
  13.1 0.0 copy-done
  13.1 11.0 %gather_fusion = bf16[2048,2048]{1,0:T(8,128)(2,1)} fusion(bf16[256,2048]{1,0:T(8,128)(2,1)S(1)} %copy-done, s32[2048]{0:T(1024)S(1)} %broadcast_clamp_fusion), kind=kCustom, calls=%fused_computation | custom fusion | bytes 16785408 | tf_op jit(solution)/shard_map/gather | solution.py:23
  24.2 0.0 all-to-all-done
  24.2 3.9 all-to-all-start.1
  28.0 0.5 broadcast.118
  28.5 0.6 reduce.4
  29.1 0.1 reshape.80
  29.2 1.1 top_k.26
  30.3 0.1 copy.32
  30.4 0.1 reshape.51
  30.5 0.1 copy.30
  30.6 0.1 copy.29
  30.7 0.1 reshape.57
  30.8 91.2 %all-to-all-done.1 = bf16[256,8,2048]{2,1,0:T(8,128)(2,1)} async-done(((bf16[256,8,2048]{2,1,0:T(8,128)(2,1)}), bf16[256,8,2048]{2,1,0:T(8,128)(2,1)}, u32[]{:S(2)}, u32[]{:S(2)}) %all-to-all-start.1) | async-done | bytes 8388640 | tf_op jit(solution)/shard_map/all_to_all | solution.py:25
  122.0 8.3 %copy.43 = bf16[8,32,8,2048]{3,2,0,1:T(8,128)(2,1)} copy(bf16[8,32,8,2048]{3,2,1,0:T(8,128)(2,1)} %bitcast.8) | data formatting | bytes 16777216 | tf_op jit(solution)/shard_map/all_to_all | solution.py:25
  130.2 10.0 %gather_fusion.2 = bf16[512,2048]{1,0:T(8,128)(2,1)S(1)} fusion(bf16[32,64,2048]{2,1,0:T(8,128)(2,1)} %bitcast.47, s32[512]{0:T(512)S(1)} %reshape.51), kind=kCustom, calls=%fused_computation.2 | custom fusion | bytes 4198400 | tf_op jit(solution)/shard_map/jit(take_along_axis)/gather | solution.py:27
  140.2 22.7 %convert_reduce_fusion.1 = (u32[16,512]{1,0:T(8,128)S(1)}, u32[16,512]{1,0:T(8,128)S(1)}, f32[32,16,512]{2,1,0:T(8,128)S(1)}) fusion(bf16[32,2048,512]{2,1,0:T(8,128)(2,1)} %param.6, bf16[32,16,2048]{2,1,0:T(8,128)(2,1)S(1)} %bitcast.49, pred[32,16]{1,0:T(8,128)(4,1)S(1)} %copy.30), kind=kOutput, calls=%fused_computation.20 | convolution fusion | flops 1077657600 | bytes 70320640 | tf_op jit(solution)/shard_map/ecd,edf->ecf/dot_general | solution.py:28
  163.0 22.8 %convolution_convert_fusion = bf16[32,16,2048]{2,1,0:T(8,128)(2,1)S(1)} fusion(bf16[32,512,2048]{2,1,0:T(8,128)(2,1)} %param.7, f32[32,16,512]{2,1,0:T(8,128)S(1)} %get-tuple-element.27, u32[16,512]{1,0:T(8,128)S(1)} %get-tuple-element.18, u32[16,512]{1,0:T(8,128)S(1)} %get-tuple-element.17), kind=kOutput, calls=%fused_computation.8 | convolution fusion | flops 1092616192 | bytes 70320128 | tf_op jit(solution)/shard_map/ecf,efd->ecd/dot_general | solution.py:29
  185.8 4.3 broadcast_in_dim.31
  190.1 93.6 %scatter_fusion = bf16[32,64,2048]{2,1,0:T(8,128)(2,1)} fusion(bf16[32,64,2048]{2,1,0:T(8,128)(2,1)} %broadcast_in_dim.31, s32[512]{0:T(512)S(1)} %reshape.57, bf16[512,2048]{1,0:T(8,128)(2,1)S(1)} %bitcast.50), kind=kCustom, calls=%fused_computation.3 | custom fusion | bytes 6295552 | tf_op jit(solution)/shard_map/scatter | solution.py:30
  283.7 11.2 %copy.33 = bf16[32,64,2048]{2,0,1:T(8,128)(2,1)} copy(bf16[32,64,2048]{2,1,0:T(8,128)(2,1)} %scatter_fusion) | data formatting | bytes 16777216 | tf_op jit(solution)/shard_map/scatter | solution.py:30
  294.9 0.0 copy-start.1
  294.9 3.8 all-to-all-start.2
  298.8 0.2 convert_element_type.25
  299.0 1.0 bitcast_or_fusion
  300.0 0.1 reshape.45
  300.1 0.0 copy-done.1
  300.1 0.1 reduce_max.9
  300.2 0.2 fusion.47
  300.4 0.1 divide_bitcast_fusion
  300.6 0.0 copy-start.3
  300.6 16.8 %gather_fusion.1 = f32[2048]{0:T(1024)S(1)} fusion(f32[256,256]{0,1:T(8,128)S(1)} %divide_bitcast_fusion, s32[2048]{0:T(1024)S(1)} %reshape.45), kind=kCustom, calls=%fused_computation.1 | custom fusion | bytes 32768 | tf_op jit(solution)/shard_map/jit(take_along_axis)/gather | solution.py:22
  317.4 0.1 reshape.48
  317.5 0.0 copy-done.3
  317.5 0.1 mul.26
  317.6 0.1 reshape.65
  317.7 75.0 %all-to-all-done.2 = bf16[32,64,2048]{2,0,1:T(8,128)(2,1)} async-done(((bf16[32,64,2048]{2,0,1:T(8,128)(2,1)}), bf16[32,64,2048]{2,0,1:T(8,128)(2,1)}, u32[]{:S(2)}, u32[]{:S(2)}) %all-to-all-start.2) | async-done | bytes 8388640 | tf_op jit(solution)/shard_map/all_to_all | solution.py:31
  392.8 13.9 %convert_bitcast_fusion = f32[8,32,8,2048]{3,2,0,1:T(8,128)} fusion(bf16[32,64,2048]{2,0,1:T(8,128)(2,1)} %all-to-all-done.2), kind=kLoop, calls=%fused_computation.5 | loop fusion | flops 4194304 | bytes 25165824 | tf_op jit(solution)/shard_map/convert_element_type | solution.py:32
  406.7 6.5 %copy.35 = f32[8,32,8,2048]{3,2,1,0:T(8,128)S(1)} copy(f32[8,32,8,2048]{3,2,0,1:T(8,128)} %convert_bitcast_fusion) | data formatting | bytes 33554432 | tf_op jit(solution)/shard_map/convert_element_type | solution.py:32
  413.3 6.9 %bitcast_multiply_fusion = f32[2048,2048]{1,0:T(8,128)} fusion(f32[8,32,8,2048]{3,2,1,0:T(8,128)S(1)} %copy.35, f32[2048]{0:T(1024)S(1)} %mul.26), kind=kLoop, calls=%fused_computation.6 | loop fusion | flops 4194304 | bytes 33562624 | tf_op jit(solution)/shard_map/mul | solution.py:32
  420.2 28.2 %scatter_fusion.1 = f32[256,2048]{1,0:T(8,128)S(1)} fusion(f32[256,2048]{1,0:T(8,128)S(1)} %convert_element_type.25, s32[2048]{0:T(1024)S(1)} %reshape.65, f32[2048,2048]{1,0:T(8,128)} %bitcast_multiply_fusion), kind=kCustom, calls=%fused_computation.4 | custom fusion | flops 4194304 | bytes 50339840 | tf_op jit(solution)/shard_map/scatter-add | solution.py:33
  448.4 1.1 convert_element_type.32
  (9 shorter events, 0.1 us)
Async XLA Ops:
  0.0 13.1 %copy-start = (bf16[256,2048]{1,0:T(8,128)(2,1)S(1)}, bf16[256,2048]{1,0:T(8,128)(2,1)}, u32[]{:S(2)}) copy-start(bf16[256,2048]{1,0:T(8,128)(2,1)} %param.4) | copy-start | bytes 3145732
  7.8 16.3 %all-to-all-start = ((f32[8,1,256]{2,1,0:T(1,128)}), f32[8,1,256]{2,1,0:T(1,128)S(1)}, u32[]{:S(2)}, u32[]{:S(2)}) async-start(f32[8,1,256]{2,1,0:T(1,128)} %reshape.79), calls=%async_computation | async-start | bytes 16384 | tf_op jit(solution)/shard_map/all_to_all | solution.py:24
  12.3 0.7 copy-start.2
  24.2 97.8 %all-to-all-start.1 = ((bf16[256,8,2048]{2,1,0:T(8,128)(2,1)}), bf16[256,8,2048]{2,1,0:T(8,128)(2,1)}, u32[]{:S(2)}, u32[]{:S(2)}) async-start(bf16[256,8,2048]{2,1,0:T(8,128)(2,1)} %bitcast.48), calls=%async_computation.1 | async-start | bytes 16777216 | tf_op jit(solution)/shard_map/all_to_all | solution.py:25
  294.9 5.1 %copy-start.1 = (f32[256,256]{1,0:T(8,128)S(1)}, f32[256,256]{1,0:T(8,128)}, u32[]{:S(2)}) copy-start(f32[256,256]{1,0:T(8,128)} %param.5) | copy-start | bytes 786436
  294.9 97.8 %all-to-all-start.2 = ((bf16[32,64,2048]{2,0,1:T(8,128)(2,1)}), bf16[32,64,2048]{2,0,1:T(8,128)(2,1)}, u32[]{:S(2)}, u32[]{:S(2)}) async-start(bf16[32,64,2048]{2,0,1:T(8,128)(2,1)} %copy.33), calls=%async_computation.2 | async-start | bytes 16777216 | tf_op jit(solution)/shard_map/all_to_all | solution.py:31
  300.6 16.9 %copy-start.3 = (s32[256,256]{1,0:T(8,128)S(1)}, s32[256,256]{1,0:T(8,128)}, u32[]{:S(2)}) copy-start(s32[256,256]{1,0:T(8,128)} %copy-done.2) | copy-start | bytes 786436
where the time goes:
time: 453 us; the launch traced here: 449 us
  waiting for transfers between devices  166 us (37%)
  local copies, waits for them, and re-layouts  165 us (36%)
  other arithmetic  60.4 us (13%)
  matrix products  45.6 us (10%)
  starting transfers between devices  12 us (3%)
    scatter x2, local copies, waits for them, and re-layouts, device_step(): jnp.zeros_like(recv_rows).at[jnp.arange(exp_dev)[:, None], sel_pos]  105 us
    all_to_all x1, waiting for transfers between devices, device_step(): recv_rows = lax.all_to_all(cand_rows, 'ep', 0, 1, tiled=True)  91.2 us
    all_to_all x1, waiting for transfers between devices, device_step(): back_out = lax.all_to_all(slot_out, 'ep', 1, 0, tiled=True)  75 us
    scatter-add x1, other arithmetic, device_step(): jax.ops.segment_sum(weighted.reshape(-1, d_model), cand_idx.reshape(-1),...  28.2 us
    dot_general x1, matrix products, device_step(): jnp.einsum('ecf,efd->ecd', hidden, w_out, preferred_element_type=jnp.floa...  22.8 us
    dot_general x1, matrix products, device_step(): jnp.einsum('ecd,edf->ecf', picked, w_in, preferred_element_type=jnp.float32)  22.7 us
    gather x3, local copies, waits for them, and re-layouts, device_step(): cand_gate = jnp.take_along_axis(gates.T, cand_idx, axis=1)  17 us
    convert_element_type x1, other arithmetic, device_step(): weighted = cand_gate[:, :, None] * back_out.astype(jnp.float32)  13.9 us
  transfers between devices with their start and end apart: 3, of which 2 were waited for; matrix products, arithmetic and copies ran while one was open for 7% of the time, Pallas kernels for 0%

commit v1 on v0

v1 whole, which is shorter than its diff:
```python
import functools

import jax
import jax.numpy as jnp
from jax import lax
from jax.experimental import pallas as pl
from jax.experimental.pallas import tpu as pltpu
from jax.sharding import PartitionSpec as P

MESH = pl.DeviceIdType.MESH
F32, BF16 = jnp.float32, jnp.bfloat16
DEV = 8
TOK = 256
D = 2048
FF = 512
EXP = 32
ALL_EXP = EXP * DEV
CAP = 16
SLOTS = EXP * CAP
NC = 8
CW = D // NC
GE = 8
NG = EXP // GE
ITEMS = NC * NG


def dot(a, b):
    return jnp.dot(a, b, preferred_element_type=F32)


def iota(shape, dim):
    return lax.broadcasted_iota(jnp.int32, shape, dim)


def gelu(v):
    return 0.5 * v * (1.0 + lax.erf(v * 0.7071067811865476))


def moe_kernel(bound, ns1, ns2, tok, logit, w1, w2, out, flag_out,
               xall, w1buf, w2buf, lt, ltr, thr_own, thr, n_own, n_par, flag_own, flags,
               slot_s, rank_s, p_s, v_s, vt_s, q_s, pick_s, hacc, h_s, zc_s, zs, recv,
               r2_s, gt_s, at_s, a_s, out_s,
               w1sem, w2sem, xsem, osem, lsend, lrecv, tsend, trecv, fsend, frecv, nsem,
               dsend, drecv, rsend, rrecv):
    me = lax.axis_index("ep")
    k = me % 2
    chip = me // 2
    cx = chip % 2
    cy = chip // 2
    dx = 2 - 4 * cx
    dy = 4 - 8 * cy
    other = 1 - 2 * k
    partner = me + other
    xn, yn, dg = me + dx, me + dy, me + dx + dy
    first = me + (1 - k) * dx + k * dy
    second = me + k * dx + (1 - k) * dy

    def rcopy(src, dst, ss, rs, dev):
        return pltpu.make_async_remote_copy(src_ref=src, dst_ref=dst, send_sem=ss, recv_sem=rs,
                                            device_id={"ep": dev}, device_id_type=MESH)

    def w1_copy(i):
        s = i % ns1
        return pltpu.make_async_copy(
            w1.at[pl.ds((i % NG) * GE, GE), pl.ds((i // NG) * CW, CW), :], w1buf.at[s], w1sem.at[s])

    def w2_copy(i):
        s = i % ns2
        return pltpu.make_async_copy(
            w2.at[pl.ds((i % NG) * GE, GE), :, pl.ds((i // NG) * CW, CW)], w2buf.at[s], w2sem.at[s])

    def x_copy(c):
        return pltpu.make_async_copy(tok.at[:, pl.ds(c * CW, CW)], xall.at[c, pl.ds(me * TOK, TOK), :], xsem.at[c])

    for c in range(NC):
        x_copy(c).start()
    for i in range(ns1):
        w1_copy(i).start()
    for i in range(ns2):
        w2_copy(i).start()

    barrier = pltpu.get_barrier_semaphore()
    for j in range(1, DEV):
        pl.semaphore_signal(barrier, inc=1, device_id={"ep": (me + j) % DEV}, device_id_type=MESH)
    lt[...] = logit[...].T
    ltr[pl.ds(me * EXP, EXP), :] = lt[pl.ds(me * EXP, EXP), :]
    pl.semaphore_wait(barrier, DEV - 1)

    def l_copy(j):
        d = (me + j) % DEV
        return rcopy(lt.at[pl.ds(d * EXP, EXP), :], ltr.at[pl.ds(me * EXP, EXP), :], lsend.at[j], lrecv.at[me], d)

    for j in range(1, DEV):
        l_copy(j).start()

    def xblk(c, d):
        return xall.at[c, pl.ds(d * TOK, TOK), :]

    def d_copy(c, block, dev, n):
        return rcopy(xblk(c, block), xblk(c, block), dsend.at[c * 7 + n], drecv.at[c * DEV + block], dev)

    def own(c):
        x_copy(c).wait()
        d_copy(c, me, first, 0).start()
        d_copy(c, me, second, 1).start()
        d_copy(c, me, partner, 2).start()

    def pump(c):
        d_copy(c, first, partner, 4).wait_recv()
        d_copy(c, first, second, 3).start()
        d_copy(c, first, partner, 4).start()

        @pl.when(c + 2 < NC)
        def _():
            own(c + 2)

        d_copy(c, second, partner, 5).wait_recv()
        d_copy(c, second, partner, 5).start()
        d_copy(c, dg, partner, 6).wait_recv()
        d_copy(c, dg, partner, 6).start()

    def partner_blocks(c):
        for d in (partner, first + other, second + other, dg + other):
            d_copy(c, d, partner, 0).wait_recv()

    own(0)
    own(1)

    for j in range(1, DEV):
        s = (me + j) % DEV
        rcopy(lt.at[pl.ds(0, EXP), :], ltr.at[pl.ds(s * EXP, EXP), :], lsend.at[j], lrecv.at[s], s).wait_recv()
    neg = jnp.float32(-jnp.inf)

    def next_max(_, m):
        acc = jnp.full((EXP, TOK), neg, F32)
        for s in range(DEV):
            v = ltr[s * EXP:(s + 1) * EXP, :]
            acc = jnp.maximum(acc, jnp.where(v < m, v, neg))
        return jnp.max(acc, axis=1, keepdims=True)

    t = lax.fori_loop(0, CAP, next_max, jnp.full((EXP, 1), jnp.inf, F32))
    thr_own[...] = jnp.broadcast_to(t, (EXP, 128))
    thr[pl.ds(me * EXP, EXP), :] = jnp.broadcast_to(t, (EXP, 128))

    def t_copy(j, src_dev):
        return rcopy(thr_own, thr.at[pl.ds(src_dev * EXP, EXP), :], tsend.at[j], trecv.at[src_dev], (me + j) % DEV)

    for j in range(1, DEV):
        t_copy(j, me).start()

    pump(0)

    tri = jnp.where(iota((TOK, TOK), 0) < iota((TOK, TOK), 1), 1.0, 0.0).astype(BF16)
    ones = jnp.ones((TOK, TOK), BF16)
    i0, i1 = iota((ALL_EXP, ALL_EXP), 0), iota((ALL_EXP, ALL_EXP), 1)
    s0, e0, s1, e1 = i0 >> 5, i0 & 31, i1 >> 5, i1 & 31
    t8 = jnp.concatenate([t] * DEV, axis=0)
    sel = ltr[...] >= t8
    mo = jnp.where(sel, 1.0, 0.0).astype(BF16)
    cnt = dot(mo, tri)
    num = dot(mo, ones).astype(BF16)
    m_slot = jnp.where((e0 == e1) & (s1 < s0), 1.0, 0.0).astype(BF16)
    m_rank = jnp.where(((s0 >> 1) == (s1 >> 1)) & ((e1 < e0) | ((e1 == e0) & (s1 < s0))), 1.0, 0.0).astype(BF16)
    slot_s[...] = jnp.where(sel, dot(m_slot, num) + cnt, -1.0)
    rank_s[...] = jnp.where(sel, dot(m_rank, num) + cnt, -1.0)

    kio = iota((CAP, TOK), 0).astype(F32)
    lio = iota((CAP, 128), 1)

    def build_p(e, _):
        acc = jnp.zeros((CAP, 128), F32)
        for ch in range(DEV // 2):
            v = jnp.zeros((CAP, TOK), F32)
            for s in (2 * ch, 2 * ch + 1):
                hit = slot_s[pl.ds(s * EXP + e, 1), :] == kio
                p_s[pl.ds(e * CAP, CAP), s * TOK:(s + 1) * TOK] = jnp.where(hit, 1.0, 0.0).astype(BF16)
                v = v + jnp.where(hit, rank_s[pl.ds(s * EXP + e, 1), :] + 1.0, 0.0)
            acc = jnp.where(lio == ch, jnp.sum(v, axis=1, keepdims=True), acc)
        v_s[pl.ds(e * CAP, CAP), :] = acc
        return 0

    lax.fori_loop(0, EXP, build_p, 0, unroll=2)
    pump(1)

    for j in range(1, DEV):
        t_copy(j, (me + j) % DEV).wait_recv()
    la = lt[...]
    sel2 = la >= jnp.concatenate([thr[...], thr[...]], axis=1)
    mt = jnp.where(sel2, 1.0, 0.0).astype(BF16)
    num2 = dot(mt, ones)
    n_own[...] = num2[:, :128]
    n_copy = rcopy(n_own, n_par, nsem.at[0], nsem.at[1], partner)
    n_copy.start()
    ex = jnp.exp(la - jnp.max(la, axis=0, keepdims=True))
    gt_s[...] = ex / jnp.sum(ex, axis=0, keepdims=True)

    vt_s[...] = v_s[...].T
    rio = iota((bound, SLOTS), 0).astype(F32) + 1.0
    for n, d in enumerate((xn, yn, dg, me)):
        q_s[n * bound:(n + 1) * bound, :] = jnp.where(vt_s[pl.ds(d // 2, 1), :] == rio, 1.0, 0.0).astype(BF16)

    n_copy.wait_recv()
    npar = jnp.concatenate([n_par[...], n_par[...]], axis=1)
    both = num2 + npar
    m_base = jnp.where((s0 == s1) & (e1 < e0), 1.0, 0.0).astype(BF16)
    base = dot(m_base, both.astype(BF16))
    r2_s[...] = jnp.where(sel2, base + dot(mt, tri) + k.astype(F32) * npar, -1.0)
    over = jnp.max(jnp.max(base + both, axis=0, keepdims=True), axis=1, keepdims=True)
    flag_own[...] = jnp.broadcast_to(jnp.where(over > bound, 1.0, 0.0), (8, 128))

    def f_copy(j, src_dev):
        return rcopy(flag_own, flags.at[src_dev], fsend.at[j], frecv.at[src_dev], (me + j) % DEV)

    for j in range(1, DEV):
        f_copy(j, me).start()
    flags[me] = flag_own[...]
    pump(2)
    hacc[...] = jnp.zeros((SLOTS, FF), F32)

    def first_product(c, last):
        partner_blocks(c)
        pick_s[...] = dot(p_s[...], xall[c]).astype(BF16)

        def group(g, _):
            i = c * NG + g
            w1_copy(i).wait()
            s = i % ns1
            for j in range(GE):
                rows = pl.ds(g * (GE * CAP) + j * CAP, CAP)
                v = hacc[rows, :] + dot(pick_s[rows, :], w1buf[s, j])
                if last:
                    h_s[rows, :] = gelu(v).astype(BF16)
                else:
                    hacc[rows, :] = v

            @pl.when(i + ns1 < ITEMS)
            def _():
                w1_copy(i + ns1).start()

            return 0

        lax.fori_loop(0, NG, group, 0)

    def early(c, _):
        first_product(c, False)
        return 0

    def later(c, _):
        pump(c)
        first_product(c, False)
        return 0

    lax.fori_loop(0, 3, early, 0)
    lax.fori_loop(3, NC - 1, later, 0)
    pump(NC - 1)
    first_product(NC - 1, True)

    def rblk(c, d):
        return recv.at[c, pl.ds(d * bound, bound), :]

    def z_copy(c, n, dev):
        src = rblk(c, me) if n == 3 else zs.at[c, pl.ds(n * bound, bound), :]
        return rcopy(src, rblk(c, me), rsend.at[c * 7 + n], rrecv.at[c * DEV + me], dev)

    def fwd_copy(c, n, block):
        return rcopy(rblk(c, block), rblk(c, block), rsend.at[c * 7 + 4 + n], rrecv.at[c * DEV + block], partner)

    def second_product(c, _):
        def group(g, _):
            i = c * NG + g
            w2_copy(i).wait()
            s = i % ns2
            for j in range(GE):
                rows = pl.ds(g * (GE * CAP) + j * CAP, CAP)
                zc_s[rows, :] = dot(h_s[rows, :], w2buf[s, j]).astype(BF16)

            @pl.when(i + ns2 < ITEMS)
            def _():
                w2_copy(i + ns2).start()

            return 0

        lax.fori_loop(0, NG, group, 0)
        zc = zc_s[...]
        zs[c] = dot(q_s[:3 * bound, :], zc).astype(BF16)
        recv[c, pl.ds(me * bound, bound), :] = dot(q_s[3 * bound:, :], zc).astype(BF16)
        for n, dev in ((2, dg), (0, xn), (1, yn), (3, partner)):
            z_copy(c, n, dev).start()
        return 0

    lax.fori_loop(0, NC, second_product, 0)

    RB = 64

    def build_a(n, _):
        o = n // (bound // RB)
        r0 = (n % (bound // RB)) * RB
        rio2 = (iota((RB, TOK), 0) + r0).astype(F32)

        def one(e, acc):
            row = pl.ds(o * EXP + e, 1)
            return jnp.where(r2_s[row, :] == rio2, gt_s[row, :], acc)

        at_s[pl.ds(o * bound + r0, RB), :] = lax.fori_loop(0, EXP, one, jnp.zeros((RB, TOK), F32), unroll=8)
        return 0

    lax.fori_loop(0, DEV * (bound // RB), build_a, 0)

    def split_a(j, _):
        a = at_s[pl.ds(j * 128, 128), :].T
        for n in range(3):
            part = a.astype(BF16)
            a_s[n, :, pl.ds(j * 128, 128)] = part
            a = a - part.astype(F32)
        return 0

    lax.fori_loop(0, DEV * bound // 128, split_a, 0)

    def forward(c):
        for n, d in enumerate((xn, yn, dg)):
            fwd_copy(c, n, d).wait_recv()
            fwd_copy(c, n, d).start()

    def out_copy(c):
        return pltpu.make_async_copy(out_s.at[c], out.at[:, pl.ds(c * CW, CW)], osem.at[c])

    def combine(c):
        for d in (partner, xn + other, yn + other, dg + other):
            fwd_copy(c, 0, d).wait_recv()
        z = recv[c]
        y = dot(a_s[2], z) + dot(a_s[1], z) + dot(a_s[0], z)
        out_s[c] = (xall[c, pl.ds(me * TOK, TOK), :].astype(F32) + y).astype(BF16)
        out_copy(c).start()

    forward(0)

    def step(c, _):
        forward(c + 1)
        combine(c)
        return 0

    lax.fori_loop(0, NC - 1, step, 0)
    combine(NC - 1)

    acc = flag_own[...]
    for j in range(1, DEV):
        s = (me + j) % DEV
        f_copy(j, s).wait_recv()
        acc = jnp.maximum(acc, flags[s])
    flag_out[...] = acc

    for j in range(1, DEV):
        l_copy(j).wait_send()
        t_copy(j, me).wait_send()
        f_copy(j, me).wait_send()
    n_copy.wait_send()

    def drain(c, _):
        for n, (block, dev) in enumerate(((me, first), (me, second), (me, partner), (first, second),
                                          (first, partner), (second, partner), (dg, partner))):
            d_copy(c, block, dev, n).wait_send()
        for n, dev in enumerate((xn, yn, dg, partner)):
            z_copy(c, n, dev).wait_send()
        for n, d in enumerate((xn, yn, dg)):
            fwd_copy(c, n, d).wait_send()
        out_copy(c).wait()
        return 0

    lax.fori_loop(0, NC, drain, 0)


def moe_call(bound, ns1, ns2, cid, tok, logit, w1, w2):
    vm = pltpu.VMEM
    sem = pltpu.SemaphoreType.DMA
    return pl.pallas_call(
        functools.partial(moe_kernel, bound, ns1, ns2),
        out_shape=(jax.ShapeDtypeStruct((TOK, D), BF16), jax.ShapeDtypeStruct((8, 128), F32)),
        in_specs=[pl.BlockSpec(memory_space=pl.ANY), pl.BlockSpec(memory_space=pltpu.VMEM),
                  pl.BlockSpec(memory_space=pl.ANY), pl.BlockSpec(memory_space=pl.ANY)],
        out_specs=(pl.BlockSpec(memory_space=pl.ANY), pl.BlockSpec(memory_space=pltpu.VMEM)),
        scratch_shapes=[
            vm((NC, DEV * TOK, CW), BF16), vm((ns1, GE, CW, FF), BF16), vm((ns2, GE, FF, CW), BF16),
            vm((ALL_EXP, TOK), F32), vm((ALL_EXP, TOK), F32), vm((EXP, 128), F32), vm((ALL_EXP, 128), F32),
            vm((ALL_EXP, 128), F32), vm((ALL_EXP, 128), F32), vm((8, 128), F32), vm((DEV, 8, 128), F32),
            vm((ALL_EXP, TOK), F32), vm((ALL_EXP, TOK), F32), vm((SLOTS, DEV * TOK), BF16),
            vm((SLOTS, 128), F32), vm((128, SLOTS), F32), vm((4 * bound, SLOTS), BF16),
            vm((SLOTS, CW), BF16), vm((SLOTS, FF), F32), vm((SLOTS, FF), BF16), vm((SLOTS, CW), BF16),
            vm((NC, 3 * bound, CW), BF16), vm((NC, DEV * bound, CW), BF16),
            vm((ALL_EXP, TOK), F32), vm((ALL_EXP, TOK), F32), vm((DEV * bound, TOK), F32),
            vm((3, TOK, DEV * bound), BF16), vm((NC, TOK, CW), BF16),
            sem((ns1,)), sem((ns2,)), sem((NC,)), sem((NC,)), sem((DEV,)), sem((DEV,)), sem((DEV,)), sem((DEV,)),
            sem((DEV,)), sem((DEV,)), sem((2,)), sem((NC * 7,)), sem((NC * DEV,)), sem((NC * 7,)), sem((NC * DEV,)),
        ],
        compiler_params=pltpu.CompilerParams(collective_id=cid, has_side_effects=True, vmem_limit_bytes=67043328),
        name=f"moe_{bound}",
    )(tok, logit, w1, w2)


def solution(mesh):
    row_spec = P(("dp", "ep"), None)
    expert_spec = P("ep", None, None)

    def device_step(tok, logit, w1, w2):
        out, flag = moe_call(192, 5, 8, 0, tok, logit, w1, w2)
        return lax.cond(flag[0, 0] > 0, lambda: moe_call(512, 2, 2, 1, tok, logit, w1, w2)[0], lambda: out)

    return jax.shard_map(device_step, mesh=mesh, in_specs=(row_spec, row_spec, expert_spec, expert_spec),
                         out_specs=row_spec, check_vma=False)
```

time: 453 us -> 126 us (0.28)
  waiting for transfers between devices: 166 us -> 0 us
  local copies, waits for them, and re-layouts: 165 us -> 3.49 us
  Pallas kernels: 0 us -> 122 us
  other arithmetic: 60.4 us -> 0 us
  matrix products: 45.6 us -> 0 us
  starting transfers between devices: 12 us -> 0 us
    all_to_all x3 -> x0, waiting for transfers between devices: 166 us -> none  [the longest x1 91.2 us: device_step(): recv_rows = lax.all_to_all(cand_rows, 'ep', 0, 1, tiled=True)]
    pallas_call x0 -> x1, Pallas kernels: none -> 122 us  [moe_call(): pl.pallas_call(functools.partial(moe_kernel, bound, ns1, ns2), out_shape=...]
    scatter x2 -> x0, local copies, waits for them, and re-layouts: 105 us -> none  [device_step(): jnp.zeros_like(recv_rows).at[jnp.arange(exp_dev)[:, None], sel_pos]]
    dot_general x2 -> x0, matrix products: 45.6 us -> none  [the longest x1 22.8 us: device_step(): jnp.einsum('ecf,efd->ecd', hidden, w_out, preferred_element_type=jnp.floa...]
    gather x5 -> x0, local copies, waits for them, and re-layouts: 38 us -> none  [the longest x3 17 us: device_step(): cand_gate = jnp.take_along_axis(gates.T, cand_idx, axis=1)]
    scatter-add x1 -> x0, other arithmetic: 28.2 us -> none  [device_step(): jax.ops.segment_sum(weighted.reshape(-1, d_model), cand_idx.reshape(-1),...]
    convert_element_type x3 -> x0, other arithmetic: 15.3 us -> none  [the longest x1 13.9 us: device_step(): weighted = cand_gate[:, :, None] * back_out.astype(jnp.float32)]
    all_to_all x3 -> x0, starting transfers between devices: 12 us -> none  [the longest x1 4.3 us: device_step(): recv_score = lax.all_to_all(cand_score, 'ep', 0, 1, tiled=True)]
  transfers between devices with their start and end apart: 3 -> 0, of which waited for: 2 -> 0; matrix products, arithmetic and copies ran while one was open for 7% -> 0% of each run, Pallas kernels for 0% -> 0%
where the time goes in v1:
time: 126 us
  Pallas kernels  122 us (97%)
  local copies, waits for them, and re-layouts  3.49 us (3%)
    pallas_call x1, Pallas kernels, moe_call(): pl.pallas_call(functools.partial(moe_kernel, bound, ns1, ns2), out_shape=...  122 us

profile of v1, /device:TPU:0, one launch (start us, length us, event | category | flops | bytes accessed | tf_op | source)
XLA Modules:
  0.0 125.9 jit_solution(12852360917067118600)
XLA Ops:
  0.0 121.5 %moe_192.1 = (bf16[256,2048]{1,0:T(8,128)(2,1)}, f32[8,128]{1,0:T(8,128)}) custom-call(bf16[256,2048]{1,0:T(8,128)(2,1)} %tok.1, f32[256,256]{1,0:T(8,128)} %logit.1, bf16[32,2048,512]{2,1,0:T(8,128)(2,1)} %w1.1, bf16[32,512,2048]{2,1,0:T(8,128)(2,1)} %w2.1), custom_call_target="tpu_custom_call" | custom-call | tf_op jit(solution)/shard_map/moe_192/pallas_call | solution.py:375
  121.5 1.2 slice.3
  123.4 0.2 conditional.1
  123.6 2.3 %copy.10 = bf16[256,2048]{1,0:T(8,128)(2,1)} copy(bf16[256,2048]{1,0:T(8,128)(2,1)} %get-tuple-element.26) | data formatting | bytes 2097152

commit v2 on v1

--- a/solution.py
+++ b/solution.py
@@ -37,7 +37,7 @@
 
 
 def moe_kernel(bound, ns1, ns2, tok, logit, w1, w2, out, flag_out,
-               xall, w1buf, w2buf, lt, ltr, thr_own, thr, n_own, n_par, flag_own, flags,
+               xall, w1buf, w2buf, log_s, lt, ltr, thr_own, thr, n_own, n_par, flag_own, flags,
                slot_s, rank_s, p_s, v_s, vt_s, q_s, pick_s, hacc, h_s, zc_s, zs, recv,
                r2_s, gt_s, at_s, a_s, out_s,
                w1sem, w2sem, xsem, osem, lsend, lrecv, tsend, trecv, fsend, frecv, nsem,
@@ -72,17 +72,15 @@
     def x_copy(c):
         return pltpu.make_async_copy(tok.at[:, pl.ds(c * CW, CW)], xall.at[c, pl.ds(me * TOK, TOK), :], xsem.at[c])
 
+    barrier = pltpu.get_barrier_semaphore()
+    for j in range(1, DEV):
+        pl.semaphore_signal(barrier, inc=1, device_id={"ep": (me + j) % DEV}, device_id_type=MESH)
+    log_copy = pltpu.make_async_copy(logit, log_s, nsem.at[2])
+    log_copy.start()
     for c in range(NC):
         x_copy(c).start()
-    for i in range(ns1):
-        w1_copy(i).start()
-    for i in range(ns2):
-        w2_copy(i).start()
-
-    barrier = pltpu.get_barrier_semaphore()
-    for j in range(1, DEV):
-        pl.semaphore_signal(barrier, inc=1, device_id={"ep": (me + j) % DEV}, device_id_type=MESH)
-    lt[...] = logit[...].T
+    log_copy.wait()
+    lt[...] = log_s[...].T
     ltr[pl.ds(me * EXP, EXP), :] = lt[pl.ds(me * EXP, EXP), :]
     pl.semaphore_wait(barrier, DEV - 1)
 
@@ -105,15 +103,16 @@
         d_copy(c, me, second, 1).start()
         d_copy(c, me, partner, 2).start()
 
-    def pump(c):
+    def relay(c):
         d_copy(c, first, partner, 4).wait_recv()
         d_copy(c, first, second, 3).start()
         d_copy(c, first, partner, 4).start()
 
-        @pl.when(c + 2 < NC)
+        @pl.when(c + 3 < NC)
         def _():
-            own(c + 2)
-
+            own(c + 3)
+
+    def share(c):
         d_copy(c, second, partner, 5).wait_recv()
         d_copy(c, second, partner, 5).start()
         d_copy(c, dg, partner, 6).wait_recv()
@@ -125,6 +124,11 @@
 
     own(0)
     own(1)
+    own(2)
+    for i in range(ns1):
+        w1_copy(i).start()
+    for i in range(ns2):
+        w2_copy(i).start()
 
     for j in range(1, DEV):
         s = (me + j) % DEV
@@ -148,7 +152,7 @@
     for j in range(1, DEV):
         t_copy(j, me).start()
 
-    pump(0)
+    relay(0)
 
     tri = jnp.where(iota((TOK, TOK), 0) < iota((TOK, TOK), 1), 1.0, 0.0).astype(BF16)
     ones = jnp.ones((TOK, TOK), BF16)
@@ -180,7 +184,8 @@
         return 0
 
     lax.fori_loop(0, EXP, build_p, 0, unroll=2)
-    pump(1)
+    relay(1)
+    share(0)
 
     for j in range(1, DEV):
         t_copy(j, (me + j) % DEV).wait_recv()
@@ -194,6 +199,9 @@
     ex = jnp.exp(la - jnp.max(la, axis=0, keepdims=True))
     gt_s[...] = ex / jnp.sum(ex, axis=0, keepdims=True)
 
+    relay(2)
+    share(1)
+
     vt_s[...] = v_s[...].T
     rio = iota((bound, SLOTS), 0).astype(F32) + 1.0
     for n, d in enumerate((xn, yn, dg, me)):
@@ -214,7 +222,6 @@
     for j in range(1, DEV):
         f_copy(j, me).start()
     flags[me] = flag_own[...]
-    pump(2)
     hacc[...] = jnp.zeros((SLOTS, FF), F32)
 
     def first_product(c, last):
@@ -241,18 +248,19 @@
 
         lax.fori_loop(0, NG, group, 0)
 
-    def early(c, _):
-        first_product(c, False)
-        return 0
-
-    def later(c, _):
-        pump(c)
-        first_product(c, False)
-        return 0
-
-    lax.fori_loop(0, 3, early, 0)
-    lax.fori_loop(3, NC - 1, later, 0)
-    pump(NC - 1)
+    def chunk(c, _):
+        relay(c)
+        share(c - 1)
+        first_product(c - 2, False)
+        return 0
+
+    relay(3)
+    share(2)
+    first_product(0, False)
+    first_product(1, False)
+    lax.fori_loop(4, NC, chunk, 0)
+    first_product(NC - 2, False)
+    share(NC - 1)
     first_product(NC - 1, True)
 
     def rblk(c, d):
@@ -375,12 +383,12 @@
     return pl.pallas_call(
         functools.partial(moe_kernel, bound, ns1, ns2),
         out_shape=(jax.ShapeDtypeStruct((TOK, D), BF16), jax.ShapeDtypeStruct((8, 128), F32)),
-        in_specs=[pl.BlockSpec(memory_space=pl.ANY), pl.BlockSpec(memory_space=pltpu.VMEM),
+        in_specs=[pl.BlockSpec(memory_space=pl.ANY), pl.BlockSpec(memory_space=pl.ANY),
                   pl.BlockSpec(memory_space=pl.ANY), pl.BlockSpec(memory_space=pl.ANY)],
         out_specs=(pl.BlockSpec(memory_space=pl.ANY), pl.BlockSpec(memory_space=pltpu.VMEM)),
         scratch_shapes=[
             vm((NC, DEV * TOK, CW), BF16), vm((ns1, GE, CW, FF), BF16), vm((ns2, GE, FF, CW), BF16),
-            vm((ALL_EXP, TOK), F32), vm((ALL_EXP, TOK), F32), vm((EXP, 128), F32), vm((ALL_EXP, 128), F32),
+            vm((TOK, ALL_EXP), F32), vm((ALL_EXP, TOK), F32), vm((ALL_EXP, TOK), F32), vm((EXP, 128), F32), vm((ALL_EXP, 128), F32),
             vm((ALL_EXP, 128), F32), vm((ALL_EXP, 128), F32), vm((8, 128), F32), vm((DEV, 8, 128), F32),
             vm((ALL_EXP, TOK), F32), vm((ALL_EXP, TOK), F32), vm((SLOTS, DEV * TOK), BF16),
             vm((SLOTS, 128), F32), vm((128, SLOTS), F32), vm((4 * bound, SLOTS), BF16),
@@ -389,7 +397,7 @@
             vm((ALL_EXP, TOK), F32), vm((ALL_EXP, TOK), F32), vm((DEV * bound, TOK), F32),
             vm((3, TOK, DEV * bound), BF16), vm((NC, TOK, CW), BF16),
             sem((ns1,)), sem((ns2,)), sem((NC,)), sem((NC,)), sem((DEV,)), sem((DEV,)), sem((DEV,)), sem((DEV,)),
-            sem((DEV,)), sem((DEV,)), sem((2,)), sem((NC * 7,)), sem((NC * DEV,)), sem((NC * 7,)), sem((NC * DEV,)),
+            sem((DEV,)), sem((DEV,)), sem((3,)), sem((NC * 7,)), sem((NC * DEV,)), sem((NC * 7,)), sem((NC * DEV,)),
         ],
         compiler_params=pltpu.CompilerParams(collective_id=cid, has_side_effects=True, vmem_limit_bytes=67043328),
         name=f"moe_{bound}",

time: 126 us -> 102 us (0.81)
  Pallas kernels: 122 us -> 97 us
    pallas_call x1, Pallas kernels: 122 us -> 97 us  [moe_call(): pl.pallas_call(functools.partial(moe_kernel, bound, ns1, ns2), out_shape=...]
where the time goes in v2:
time: 102 us; the launch traced here: 101 us
  Pallas kernels  97 us (95%)
  local copies, waits for them, and re-layouts  3.49 us (3%)
    pallas_call x1, Pallas kernels, moe_call(): pl.pallas_call(functools.partial(moe_kernel, bound, ns1, ns2), out_shape=...  97 us
    unnamed x1, local copies, waits for them, and re-layouts  2.3 us

profile of v2, /device:TPU:0, one launch (start us, length us, event | category | flops | bytes accessed | tf_op | source)
XLA Modules:
  0.0 101.4 jit_solution(13163080305344564965)
XLA Ops:
  0.0 97.0 %moe_192.1 = (bf16[256,2048]{1,0:T(8,128)(2,1)}, f32[8,128]{1,0:T(8,128)}) custom-call(bf16[256,2048]{1,0:T(8,128)(2,1)} %tok.1, f32[256,256]{1,0:T(8,128)} %logit.1, bf16[32,2048,512]{2,1,0:T(8,128)(2,1)} %w1.1, bf16[32,512,2048]{2,1,0:T(8,128)(2,1)} %w2.1), custom_call_target="tpu_custom_call" | custom-call | tf_op jit(solution)/shard_map/moe_192/pallas_call | solution.py:383
  97.1 1.2 %slice.3 = f32[1,1]{1,0:T(1,128)} slice(f32[8,128]{1,0:T(8,128)} %get-tuple-element.24), slice={[0:1], [0:1]} | slice | bytes 8 | tf_op jit(solution)/shard_map/slice | solution.py:413
  98.9 0.2 conditional.1
  99.1 2.3 %copy.10 = bf16[256,2048]{1,0:T(8,128)(2,1)} copy(bf16[256,2048]{1,0:T(8,128)(2,1)} %get-tuple-element.26) | data formatting | bytes 2097152

commit v3 on v2

v3 whole, which is shorter than its diff:
```python
import functools

import jax
import jax.numpy as jnp
from jax import lax
from jax.experimental import pallas as pl
from jax.experimental.pallas import tpu as pltpu
from jax.sharding import PartitionSpec as P

MESH = pl.DeviceIdType.MESH
F32, BF16 = jnp.float32, jnp.bfloat16
DEV = 8
TOK = 256
D = 2048
FF = 512
EXP = 32
ALL_EXP = EXP * DEV
CAP = 16
SLOTS = EXP * CAP
NC = 8
CW = D // NC
GE = 8
NG = EXP // GE
ITEMS = NC * NG


def dot(a, b):
    return jnp.dot(a, b, preferred_element_type=F32)


def iota(shape, dim):
    return lax.broadcasted_iota(jnp.int32, shape, dim)


def gelu(v):
    return 0.5 * v * (1.0 + lax.erf(v * 0.7071067811865476))


def dot_nt(a, b):
    return lax.dot_general(a, b, (((1,), (1,)), ((), ())), preferred_element_type=F32)


def onehot(cond):
    return jnp.where(cond, 1.0, 0.0).astype(BF16)


def moe_kernel(xb, nx, bound, ns1, ns2, tok, logit, w1, w2, out, flag_out,
               xr, xs, w1buf, w2buf, log_s, cand, cands, rk, rks, rt_s, w_s, c64_s,
               p_s, v_s, vt_s, q_s, pick_s, hacc, h_s, zc_s, zs, recv,
               r2_s, gt_s, at_s, a_s, out_s,
               w1sem, w2sem, xsem, osem, csend, crecv, ksend, krecv, nsem,
               dsend, drecv, rsend, rrecv):
    me = lax.axis_index("ep")
    k = me % 2
    chip = me // 2
    cx = chip % 2
    cy = chip // 2
    dx = 2 - 4 * cx
    dy = 4 - 8 * cy
    other = 1 - 2 * k
    partner = me + other
    xn, yn, dg = me + dx, me + dy, me + dx + dy
    far = (xn, yn, dg)
    neg = jnp.float32(-jnp.inf)

    def rcopy(src, dst, ss, rs, dev):
        return pltpu.make_async_remote_copy(src_ref=src, dst_ref=dst, send_sem=ss, recv_sem=rs,
                                            device_id={"ep": dev}, device_id_type=MESH)

    def w1_copy(i):
        s = i % ns1
        return pltpu.make_async_copy(
            w1.at[pl.ds((i % NG) * GE, GE), pl.ds((i // NG) * CW, CW), :], w1buf.at[s], w1sem.at[s])

    def w2_copy(i):
        s = i % ns2
        return pltpu.make_async_copy(
            w2.at[pl.ds((i % NG) * GE, GE), :, pl.ds((i // NG) * CW, CW)], w2buf.at[s], w2sem.at[s])

    def xown(c, core):
        return xr.at[c, pl.ds(core * TOK, TOK), :]

    def xlist(c, n, core):
        return xr.at[c, pl.ds(2 * TOK + (2 * n + core) * xb, xb), :]

    def x_copy(c):
        return pltpu.make_async_copy(tok.at[:, pl.ds(c * CW, CW)], xown(c, k), xsem.at[c])

    def p_copy(c, core):
        return rcopy(xown(c, core), xown(c, core), dsend.at[c * 7 + 6], drecv.at[c * DEV + 6], partner)

    def x_send(c, n):
        return rcopy(xs.at[c, pl.ds(n * xb, xb), :], xlist(c, n, k), dsend.at[c * 7 + n],
                     drecv.at[c * DEV + 2 * n + k], far[n])

    def x_fwd(c, n, core):
        return rcopy(xlist(c, n, core), xlist(c, n, core), dsend.at[c * 7 + 3 + n],
                     drecv.at[c * DEV + 2 * n + core], partner)

    barrier = pltpu.get_barrier_semaphore()
    for j in range(1, DEV):
        pl.semaphore_signal(barrier, inc=1, device_id={"ep": (me + j) % DEV}, device_id_type=MESH)
    log_copy = pltpu.make_async_copy(logit, log_s, nsem.at[0])
    log_copy.start()
    for c in range(NC):
        x_copy(c).start()
    log_copy.wait()

    def next_top(n, m):
        v = log_s[...]
        m = jnp.max(jnp.where(v < m, v, neg), axis=0, keepdims=True)
        cand[pl.ds(n, 1), :] = m
        return m

    lax.fori_loop(0, 8, next_top, jnp.full((1, ALL_EXP), jnp.inf, F32))
    pl.semaphore_wait(barrier, DEV - 1)

    def c_copy(j, src):
        return rcopy(cand, cands.at[pl.ds(src * 8, 8), :], csend.at[j], crecv.at[src], (me + j) % DEV)

    def k_copy(j, src):
        return rcopy(rk, rks.at[pl.ds(src * 8, 8), :], ksend.at[j], krecv.at[src], (me + j) % DEV)

    for j in range(1, DEV):
        c_copy(j, me).start()
    cands[pl.ds(me * 8, 8), :] = cand[...]

    def start_own(c, _):
        x_copy(c).wait()
        p_copy(c, k).start()
        return 0

    lax.fori_loop(0, NC, start_own, 0)
    if nx > 2 * TOK + 6 * xb:
        for c in range(NC):
            xr[c, 2 * TOK + 6 * xb:, :] = jnp.zeros((nx - 2 * TOK - 6 * xb, CW), BF16)
    t0, t1 = iota((TOK, TOK), 0), iota((TOK, TOK), 1)
    tri = onehot(t0 < t1)
    for j in range(1, DEV):
        c_copy(j, (me + j) % DEV).wait_recv()

    def next_max(_, m):
        v = cands[...]
        return jnp.max(jnp.where(v < m, v, neg), axis=0, keepdims=True)

    thr = lax.fori_loop(0, CAP, next_max, jnp.full((1, ALL_EXP), jnp.inf, F32))

    mo = onehot(log_s[...] >= thr)
    of_chip = onehot((iota((16, ALL_EXP), 1) >> 6) == iota((16, ALL_EXP), 0))
    used = dot_nt(of_chip, mo) > 0.5
    rt_s[...] = jnp.where(used, dot(onehot(used), tri), -1.0)
    xio = iota((xb, TOK), 0).astype(F32)
    for n in range(3):
        w_s[n * xb:(n + 1) * xb, :] = onehot(rt_s[pl.ds(far[n] // 2, 1), :] == xio)

    def compact(c, _):
        xs[c] = dot(w_s[...], xr[c, pl.ds(k * TOK, TOK), :]).astype(BF16)
        for n in (2, 0, 1):
            x_send(c, n).start()
        return 0

    lax.fori_loop(0, NC, compact, 0)
    for i in range(ns1):
        w1_copy(i).start()
    for i in range(ns2):
        w2_copy(i).start()

    of_chip2 = onehot((iota((ALL_EXP, 128), 0) >> 6) == iota((ALL_EXP, 128), 1))
    used2 = onehot(dot(mo, of_chip2) > 0.5)
    place = dot(onehot(t1 < t0), used2)
    place = jnp.where(iota((TOK, 128), 1) == chip, iota((TOK, 128), 0).astype(F32), place)
    place = dot_nt(place.astype(BF16), of_chip2)
    c64_s[...] = place

    def top_place(n, _):
        hit = log_s[...] == cand[pl.ds(n, 1), :]
        rk[pl.ds(n, 1), :] = jnp.max(jnp.where(hit, c64_s[...], -1.0), axis=0, keepdims=True)
        return 0

    lax.fori_loop(0, 8, top_place, 0)
    for j in range(1, DEV):
        k_copy(j, me).start()
    rks[pl.ds(me * 8, 8), :] = rk[...]

    cv = cands[...]
    sel = cv >= thr
    so = onehot(sel)
    j0, j1 = iota((64, 64), 0), iota((64, 64), 1)
    slot = dot(onehot(j1 < j0), so)
    inside = dot(onehot((j1 < j0) & ((j1 >> 4) == (j0 >> 4))), so)
    num = dot(onehot((j1 >> 4) == (j0 >> 4)), so)
    base = dot(num.astype(BF16), onehot((t0 < t1) & ((t0 >> 5) == (t1 >> 5))))
    rank = base + inside
    over = jnp.max(jnp.max(base + num, axis=0, keepdims=True), axis=1, keepdims=True) > bound
    c64_s[:64, :] = jnp.where(sel, rank, -1.0)

    pair = jnp.full((TOK, ALL_EXP), -1.0, F32)
    for n in range(8):
        pair = jnp.where(log_s[...] == cand[n:n + 1, :], c64_s[pl.ds(me * 8 + n, 1), :], pair)
    r2_s[...] = pair.T
    la = log_s[...].T
    ex = jnp.exp(la - jnp.max(la, axis=0, keepdims=True))
    gt_s[...] = ex / jnp.sum(ex, axis=0, keepdims=True)

    for j in range(1, DEV):
        k_copy(j, (me + j) % DEV).wait_recv()
    rv = rks[...]
    src = iota((64, ALL_EXP), 0) >> 3
    exp_chip = iota((64, ALL_EXP), 1) >> 6
    wide = jnp.max(jnp.max(jnp.where(sel & ((src >> 1) != exp_chip), rv, -1.0), axis=0, keepdims=True),
                   axis=1, keepdims=True) >= xb
    flag_out[...] = jnp.broadcast_to(jnp.where(over | wide, 1.0, 0.0), (8, 128))
    rel = (src >> 1) ^ chip
    start = jnp.where(rel == 0, (src & 1) * TOK, 2 * TOK + (2 * (rel - 1) + (src & 1)) * xb).astype(F32)
    pos = start + rv + 1.0
    code = ((src >> 1) * 1024).astype(F32) + rank + 1.0
    pos_rows, code_rows = [], []
    for i in range(CAP):
        hit = sel & (slot == i)
        pos_rows.append(jnp.sum(jnp.where(hit, pos, 0.0), axis=0, keepdims=True))
        code_rows.append(jnp.sum(jnp.where(hit, code, 0.0), axis=0, keepdims=True))
    turn = ALL_EXP - me * EXP
    pos = pltpu.roll(jnp.concatenate(pos_rows, axis=0), turn, 1)
    code = pltpu.roll(jnp.concatenate(code_rows, axis=0), turn, 1)
    pio = iota((CAP, nx), 1).astype(F32) + 1.0
    for e in range(EXP):
        p_s[e * CAP:(e + 1) * CAP, :] = onehot(pos[:, e:e + 1] == pio)
        v_s[e * CAP:(e + 1) * CAP, :] = jnp.broadcast_to(code[:, e:e + 1], (CAP, 128))
    vt_s[...] = v_s[...].T[:8, :]
    rio = iota((bound, SLOTS), 0)
    for n, d in enumerate((xn, yn, dg, me)):
        want = (rio + ((d // 2) * 1024 + 1)).astype(F32)
        q_s[n * bound:(n + 1) * bound, :] = onehot(vt_s[0:1, :] == want)
    hacc[...] = jnp.zeros((SLOTS, FF), F32)

    def x_forward(c):
        for n in range(3):
            x_fwd(c, n, k).wait_recv()
            x_fwd(c, n, k).start()

    def first_product(c, last):
        for n in range(3):
            x_fwd(c, n, 1 - k).wait_recv()
        p_copy(c, 1 - k).wait_recv()
        pick_s[...] = dot(p_s[...], xr[c]).astype(BF16)

        def group(g, _):
            i = c * NG + g
            w1_copy(i).wait()
            s = i % ns1
            for j in range(GE):
                rows = pl.ds(g * (GE * CAP) + j * CAP, CAP)
                v = hacc[rows, :] + dot(pick_s[rows, :], w1buf[s, j])
                if last:
                    h_s[rows, :] = gelu(v).astype(BF16)
                else:
                    hacc[rows, :] = v

            @pl.when(i + ns1 < ITEMS)
            def _():
                w1_copy(i + ns1).start()

            return 0

        lax.fori_loop(0, NG, group, 0)

    def chunk(c, _):
        x_forward(c + 1)
        first_product(c, False)
        return 0

    x_forward(0)
    lax.fori_loop(0, NC - 1, chunk, 0)
    first_product(NC - 1, True)

    def rblk(c, d):
        return recv.at[c, pl.ds(d * bound, bound), :]

    def z_copy(c, n, dev):
        src = rblk(c, me) if n == 3 else zs.at[c, pl.ds(n * bound, bound), :]
        return rcopy(src, rblk(c, me), rsend.at[c * 7 + n], rrecv.at[c * DEV + me], dev)

    def fwd_copy(c, n, block):
        return rcopy(rblk(c, block), rblk(c, block), rsend.at[c * 7 + 4 + n], rrecv.at[c * DEV + block], partner)

    def second_product(c, _):
        def group(g, _):
            i = c * NG + g
            w2_copy(i).wait()
            s = i % ns2
            for j in range(GE):
                rows = pl.ds(g * (GE * CAP) + j * CAP, CAP)
                zc_s[rows, :] = dot(h_s[rows, :], w2buf[s, j]).astype(BF16)

            @pl.when(i + ns2 < ITEMS)
            def _():
                w2_copy(i + ns2).start()

            return 0

        lax.fori_loop(0, NG, group, 0)
        zc = zc_s[...]
        zs[c] = dot(q_s[:3 * bound, :], zc).astype(BF16)
        recv[c, pl.ds(me * bound, bound), :] = dot(q_s[3 * bound:, :], zc).astype(BF16)
        for n, dev in ((2, dg), (0, xn), (1, yn), (3, partner)):
            z_copy(c, n, dev).start()
        return 0

    lax.fori_loop(0, NC, second_product, 0)

    RB = 64

    def build_a(n, _):
        o = n // (bound // RB)
        r0 = (n % (bound // RB)) * RB
        rio2 = (iota((RB, TOK), 0) + r0).astype(F32)

        def one(e, acc):
            row = pl.ds(o * EXP + e, 1)
            return jnp.where(r2_s[row, :] == rio2, gt_s[row, :], acc)

        at_s[pl.ds(o * bound + r0, RB), :] = lax.fori_loop(0, EXP, one, jnp.zeros((RB, TOK), F32), unroll=8)
        return 0

    lax.fori_loop(0, DEV * (bound // RB), build_a, 0)

    def split_a(j, _):
        a = at_s[pl.ds(j * 128, 128), :].T
        for n in range(3):
            part = a.astype(BF16)
            a_s[n, :, pl.ds(j * 128, 128)] = part
            a = a - part.astype(F32)
        return 0

    lax.fori_loop(0, DEV * bound // 128, split_a, 0)

    def forward(c):
        for n, d in enumerate((xn, yn, dg)):
            fwd_copy(c, n, d).wait_recv()
            fwd_copy(c, n, d).start()

    def out_copy(c):
        return pltpu.make_async_copy(out_s.at[c], out.at[:, pl.ds(c * CW, CW)], osem.at[c])

    def combine(c):
        for d in (partner, xn + other, yn + other, dg + other):
            fwd_copy(c, 0, d).wait_recv()
        z = recv[c]
        y = dot(a_s[2], z) + dot(a_s[1], z) + dot(a_s[0], z)
        out_s[c] = (xr[c, pl.ds(k * TOK, TOK), :].astype(F32) + y).astype(BF16)
        out_copy(c).start()

    forward(0)

    def step(c, _):
        forward(c + 1)
        combine(c)
        return 0

    lax.fori_loop(0, NC - 1, step, 0)
    combine(NC - 1)

    for j in range(1, DEV):
        c_copy(j, me).wait_send()
        k_copy(j, me).wait_send()

    def drain(c, _):
        p_copy(c, k).wait_send()
        for n in range(3):
            x_send(c, n).wait_send()
            x_fwd(c, n, k).wait_send()
        for n, dev in enumerate((xn, yn, dg, partner)):
            z_copy(c, n, dev).wait_send()
        for n, d in enumerate((xn, yn, dg)):
            fwd_copy(c, n, d).wait_send()
        out_copy(c).wait()
        return 0

    lax.fori_loop(0, NC, drain, 0)


def moe_call(xb, bound, ns1, ns2, cid, tok, logit, w1, w2):
    nx = -(-(2 * TOK + 6 * xb) // 128) * 128
    vm = pltpu.VMEM
    sem = pltpu.SemaphoreType.DMA
    sq = vm((ALL_EXP, TOK), F32)
    return pl.pallas_call(
        functools.partial(moe_kernel, xb, nx, bound, ns1, ns2),
        out_shape=(jax.ShapeDtypeStruct((TOK, D), BF16), jax.ShapeDtypeStruct((8, 128), F32)),
        in_specs=[pl.BlockSpec(memory_space=pl.ANY)] * 4,
        out_specs=(pl.BlockSpec(memory_space=pl.ANY), pl.BlockSpec(memory_space=pltpu.VMEM)),
        scratch_shapes=[
            vm((NC, nx, CW), BF16), vm((NC, 3 * xb, CW), BF16),
            vm((ns1, GE, CW, FF), BF16), vm((ns2, GE, FF, CW), BF16),
            sq, vm((8, ALL_EXP), F32), vm((64, ALL_EXP), F32), vm((8, ALL_EXP), F32), vm((64, ALL_EXP), F32),
            vm((16, TOK), F32), vm((3 * xb, TOK), BF16), sq,
            vm((SLOTS, nx), BF16), vm((SLOTS, 128), F32), vm((8, SLOTS), F32), vm((4 * bound, SLOTS), BF16),
            vm((SLOTS, CW), BF16), vm((SLOTS, FF), F32), vm((SLOTS, FF), BF16), vm((SLOTS, CW), BF16),
            vm((NC, 3 * bound, CW), BF16), vm((NC, DEV * bound, CW), BF16),
            sq, sq, vm((DEV * bound, TOK), F32), vm((3, TOK, DEV * bound), BF16), vm((NC, TOK, CW), BF16),
            sem((ns1,)), sem((ns2,)), sem((NC,)), sem((NC,)), sem((DEV,)), sem((DEV,)), sem((DEV,)), sem((DEV,)),
            sem((1,)), sem((NC * 7,)), sem((NC * DEV,)), sem((NC * 7,)), sem((NC * DEV,)),
        ],
        compiler_params=pltpu.CompilerParams(collective_id=cid, has_side_effects=True, vmem_limit_bytes=67043328),
        name=f"moe_{bound}",
    )(tok, logit, w1, w2)


def solution(mesh):
    row_spec = P(("dp", "ep"), None)
    expert_spec = P("ep", None, None)

    def device_step(tok, logit, w1, w2):
        out, flag = moe_call(144, 192, 5, 8, 0, tok, logit, w1, w2)
        return lax.cond(flag[0, 0] > 0, lambda: moe_call(TOK, 512, 2, 2, 1, tok, logit, w1, w2)[0], lambda: out)

    return jax.shard_map(device_step, mesh=mesh, in_specs=(row_spec, row_spec, expert_spec, expert_spec),
                         out_specs=row_spec, check_vma=False)
```

time: 102 us -> 106 us (1.039)
  Pallas kernels: 97 us -> 101 us
    pallas_call x1, Pallas kernels: 97 us -> 101 us  [moe_call(): pl.pallas_call(functools.partial(moe_kernel, xb, nx, bound, ns1, ns2), ou...]
where the time goes in v3:
time: 106 us; the launch traced here: 105 us
  Pallas kernels  101 us (95%)
  local copies, waits for them, and re-layouts  3.49 us (3%)
    pallas_call x1, Pallas kernels, moe_call(): pl.pallas_call(functools.partial(moe_kernel, xb, nx, bound, ns1, ns2), ou...  101 us
    unnamed x1, local copies, waits for them, and re-layouts  2.3 us

profile of v3, /device:TPU:0, one launch (start us, length us, event | category | flops | bytes accessed | tf_op | source)
XLA Modules:
  0.0 105.4 jit_solution(8721173545471338512)
XLA Ops:
  0.0 101.0 %moe_192.1 = (bf16[256,2048]{1,0:T(8,128)(2,1)}, f32[8,128]{1,0:T(8,128)}) custom-call(bf16[256,2048]{1,0:T(8,128)(2,1)} %tok.1, f32[256,256]{1,0:T(8,128)} %logit.1, bf16[32,2048,512]{2,1,0:T(8,128)(2,1)} %w1.1, bf16[32,512,2048]{2,1,0:T(8,128)(2,1)} %w2.1), custom_call_target="tpu_custom_call" | custom-call | tf_op jit(solution)/shard_map/moe_192/pallas_call | solution.py:387
  101.0 1.2 %slice.3 = f32[1,1]{1,0:T(1,128)} slice(f32[8,128]{1,0:T(8,128)} %get-tuple-element.24), slice={[0:1], [0:1]} | slice | bytes 8 | tf_op jit(solution)/shard_map/slice | solution.py:415
  102.9 0.2 conditional.1
  103.1 2.3 %copy.10 = bf16[256,2048]{1,0:T(8,128)(2,1)} copy(bf16[256,2048]{1,0:T(8,128)(2,1)} %get-tuple-element.26) | data formatting | bytes 2097152

commit v4 on v3

--- a/solution.py
+++ b/solution.py
@@ -159,11 +159,7 @@
             x_send(c, n).start()
         return 0
 
-    lax.fori_loop(0, NC, compact, 0)
-    for i in range(ns1):
-        w1_copy(i).start()
-    for i in range(ns2):
-        w2_copy(i).start()
+    compact(0, 0)
 
     of_chip2 = onehot((iota((ALL_EXP, 128), 0) >> 6) == iota((ALL_EXP, 128), 1))
     used2 = onehot(dot(mo, of_chip2) > 0.5)
@@ -181,6 +177,11 @@
     for j in range(1, DEV):
         k_copy(j, me).start()
     rks[pl.ds(me * 8, 8), :] = rk[...]
+    lax.fori_loop(1, NC, compact, 0)
+    for i in range(ns1):
+        w1_copy(i).start()
+    for i in range(ns2):
+        w2_copy(i).start()
 
     cv = cands[...]
     sel = cv >= thr

time: 106 us -> 87.9 us (0.83)
  Pallas kernels: 101 us -> 83.4 us
    pallas_call x1, Pallas kernels: 101 us -> 83.4 us  [moe_call(): pl.pallas_call(functools.partial(moe_kernel, xb, nx, bound, ns1, ns2), ou...]
where the time goes in v4:
time: 87.9 us; the launch traced here: 87.7 us
  Pallas kernels  83.4 us (95%)
  local copies, waits for them, and re-layouts  3.49 us (4%)
    pallas_call x1, Pallas kernels, moe_call(): pl.pallas_call(functools.partial(moe_kernel, xb, nx, bound, ns1, ns2), ou...  83.4 us
    unnamed x1, local copies, waits for them, and re-layouts  2.3 us

profile of v4, /device:TPU:0, one launch (start us, length us, event | category | flops | bytes accessed | tf_op | source)
XLA Modules:
  0.0 87.7 jit_solution(12289275597211472945)
XLA Ops:
  0.0 83.4 %moe_192.1 = (bf16[256,2048]{1,0:T(8,128)(2,1)}, f32[8,128]{1,0:T(8,128)}) custom-call(bf16[256,2048]{1,0:T(8,128)(2,1)} %tok.1, f32[256,256]{1,0:T(8,128)} %logit.1, bf16[32,2048,512]{2,1,0:T(8,128)(2,1)} %w1.1, bf16[32,512,2048]{2,1,0:T(8,128)(2,1)} %w2.1), custom_call_target="tpu_custom_call" | custom-call | tf_op jit(solution)/shard_map/moe_192/pallas_call | solution.py:388
  83.4 1.2 %slice.3 = f32[1,1]{1,0:T(1,128)} slice(f32[8,128]{1,0:T(8,128)} %get-tuple-element.24), slice={[0:1], [0:1]} | slice | bytes 8 | tf_op jit(solution)/shard_map/slice | solution.py:416
  85.2 0.2 conditional.1
  85.4 2.3 %copy.10 = bf16[256,2048]{1,0:T(8,128)(2,1)} copy(bf16[256,2048]{1,0:T(8,128)(2,1)} %get-tuple-element.26) | data formatting | bytes 2097152

commit v5 on v4

--- a/solution.py
+++ b/solution.py
@@ -210,7 +210,7 @@
     exp_chip = iota((64, ALL_EXP), 1) >> 6
     wide = jnp.max(jnp.max(jnp.where(sel & ((src >> 1) != exp_chip), rv, -1.0), axis=0, keepdims=True),
                    axis=1, keepdims=True) >= xb
-    flag_out[...] = jnp.broadcast_to(jnp.where(over | wide, 1.0, 0.0), (8, 128))
+    flag_out[0, 0] = jnp.max(jnp.where(over | wide, 1.0, 0.0)).astype(jnp.int32)
     rel = (src >> 1) ^ chip
     start = jnp.where(rel == 0, (src & 1) * TOK, 2 * TOK + (2 * (rel - 1) + (src & 1)) * xb).astype(F32)
     pos = start + rv + 1.0
@@ -246,24 +246,25 @@
         pick_s[...] = dot(p_s[...], xr[c]).astype(BF16)
 
         def group(g, _):
-            i = c * NG + g
+            i = c * NG + 2 * g
             w1_copy(i).wait()
-            s = i % ns1
-            for j in range(GE):
-                rows = pl.ds(g * (GE * CAP) + j * CAP, CAP)
-                v = hacc[rows, :] + dot(pick_s[rows, :], w1buf[s, j])
+            w1_copy(i + 1).wait()
+            for j in range(2 * GE):
+                rows = pl.ds(g * (2 * GE * CAP) + j * CAP, CAP)
+                v = hacc[rows, :] + dot(pick_s[rows, :], w1buf[(i + j // GE) % ns1, j % GE])
                 if last:
                     h_s[rows, :] = gelu(v).astype(BF16)
                 else:
                     hacc[rows, :] = v
 
-            @pl.when(i + ns1 < ITEMS)
-            def _():
-                w1_copy(i + ns1).start()
+            for n in (i, i + 1):
+                @pl.when(n + ns1 < ITEMS)
+                def _():
+                    w1_copy(n + ns1).start()
 
             return 0
 
-        lax.fori_loop(0, NG, group, 0)
+        lax.fori_loop(0, NG // 2, group, 0)
 
     def chunk(c, _):
         x_forward(c + 1)
@@ -286,20 +287,21 @@
 
     def second_product(c, _):
         def group(g, _):
-            i = c * NG + g
+            i = c * NG + 2 * g
             w2_copy(i).wait()
-            s = i % ns2
-            for j in range(GE):
-                rows = pl.ds(g * (GE * CAP) + j * CAP, CAP)
-                zc_s[rows, :] = dot(h_s[rows, :], w2buf[s, j]).astype(BF16)
-
-            @pl.when(i + ns2 < ITEMS)
-            def _():
-                w2_copy(i + ns2).start()
+            w2_copy(i + 1).wait()
+            for j in range(2 * GE):
+                rows = pl.ds(g * (2 * GE * CAP) + j * CAP, CAP)
+                zc_s[rows, :] = dot(h_s[rows, :], w2buf[(i + j // GE) % ns2, j % GE]).astype(BF16)
+
+            for n in (i, i + 1):
+                @pl.when(n + ns2 < ITEMS)
+                def _():
+                    w2_copy(n + ns2).start()
 
             return 0
 
-        lax.fori_loop(0, NG, group, 0)
+        lax.fori_loop(0, NG // 2, group, 0)
         zc = zc_s[...]
         zs[c] = dot(q_s[:3 * bound, :], zc).astype(BF16)
         recv[c, pl.ds(me * bound, bound), :] = dot(q_s[3 * bound:, :], zc).astype(BF16)
@@ -351,33 +353,42 @@
         out_s[c] = (xr[c, pl.ds(k * TOK, TOK), :].astype(F32) + y).astype(BF16)
         out_copy(c).start()
 
-    forward(0)
-
-    def step(c, _):
-        forward(c + 1)
-        combine(c)
-        return 0
-
-    lax.fori_loop(0, NC - 1, step, 0)
-    combine(NC - 1)
-
     for j in range(1, DEV):
         c_copy(j, me).wait_send()
         k_copy(j, me).wait_send()
 
-    def drain(c, _):
+    def drain_x(c, _):
         p_copy(c, k).wait_send()
         for n in range(3):
             x_send(c, n).wait_send()
             x_fwd(c, n, k).wait_send()
+        return 0
+
+    lax.fori_loop(0, NC, drain_x, 0)
+
+    def drain_z(c):
         for n, dev in enumerate((xn, yn, dg, partner)):
             z_copy(c, n, dev).wait_send()
         for n, d in enumerate((xn, yn, dg)):
             fwd_copy(c, n, d).wait_send()
         out_copy(c).wait()
-        return 0
-
-    lax.fori_loop(0, NC, drain, 0)
+
+    forward(0)
+
+    def step(c, _):
+        forward(c + 1)
+        combine(c)
+
+        @pl.when(c > 0)
+        def _():
+            drain_z(c - 1)
+
+        return 0
+
+    lax.fori_loop(0, NC - 1, step, 0)
+    combine(NC - 1)
+    drain_z(NC - 2)
+    drain_z(NC - 1)
 
 
 def moe_call(xb, bound, ns1, ns2, cid, tok, logit, w1, w2):
@@ -387,9 +398,9 @@
     sq = vm((ALL_EXP, TOK), F32)
     return pl.pallas_call(
         functools.partial(moe_kernel, xb, nx, bound, ns1, ns2),
-        out_shape=(jax.ShapeDtypeStruct((TOK, D), BF16), jax.ShapeDtypeStruct((8, 128), F32)),
+        out_shape=(jax.ShapeDtypeStruct((TOK, D), BF16), jax.ShapeDtypeStruct((1, 1), jnp.int32)),
         in_specs=[pl.BlockSpec(memory_space=pl.ANY)] * 4,
-        out_specs=(pl.BlockSpec(memory_space=pl.ANY), pl.BlockSpec(memory_space=pltpu.VMEM)),
+        out_specs=(pl.BlockSpec(memory_space=pl.ANY), pl.BlockSpec(memory_space=pltpu.SMEM)),
         scratch_shapes=[
             vm((NC, nx, CW), BF16), vm((NC, 3 * xb, CW), BF16),
             vm((ns1, GE, CW, FF), BF16), vm((ns2, GE, FF, CW), BF16),
@@ -412,8 +423,8 @@
     expert_spec = P("ep", None, None)
 
     def device_step(tok, logit, w1, w2):
-        out, flag = moe_call(144, 192, 5, 8, 0, tok, logit, w1, w2)
-        return lax.cond(flag[0, 0] > 0, lambda: moe_call(TOK, 512, 2, 2, 1, tok, logit, w1, w2)[0], lambda: out)
+        out, flag = moe_call(144, 192, 8, 8, 0, tok, logit, w1, w2)
+        return lax.switch(flag[0, 0], (lambda: out, lambda: moe_call(TOK, 512, 2, 2, 1, tok, logit, w1, w2)[0]))
 
     return jax.shard_map(device_step, mesh=mesh, in_specs=(row_spec, row_spec, expert_spec, expert_spec),
                          out_specs=row_spec, check_vma=False)

time: 87.9 us -> 86.2 us (0.981)
  local copies, waits for them, and re-layouts: 3.49 us -> 2.3 us
    slice x1 -> x0, local copies, waits for them, and re-layouts: 1.19 us -> none  [device_step(): flag[0, 0] > 0]
where the time goes in v5:
time: 86.2 us; the launch traced here: 86 us
  Pallas kernels  82.9 us (96%)
  local copies, waits for them, and re-layouts  2.3 us (3%)
    pallas_call x1, Pallas kernels, moe_call(): pl.pallas_call(functools.partial(moe_kernel, xb, nx, bound, ns1, ns2), ou...  82.9 us
    unnamed x1, local copies, waits for them, and re-layouts  2.3 us

profile of v5, /device:TPU:0, one launch (start us, length us, event | category | flops | bytes accessed | tf_op | source)
XLA Modules:
  0.0 86.0 jit_solution(18050651495639746724)
XLA Ops:
  0.0 82.9 %moe_192.1 = (bf16[256,2048]{1,0:T(8,128)(2,1)}, s32[1,1]{1,0:T(1,128)}) custom-call(bf16[256,2048]{1,0:T(8,128)(2,1)} %tok.1, f32[256,256]{1,0:T(8,128)} %logit.1, bf16[32,2048,512]{2,1,0:T(8,128)(2,1)} %w1.1, bf16[32,512,2048]{2,1,0:T(8,128)(2,1)} %w2.1), custom_call_target="tpu_custom_call" | custom-call | tf_op jit(solution)/shard_map/moe_192/pallas_call | solution.py:399
  83.5 0.2 conditional.1
  83.7 2.3 %copy.10 = bf16[256,2048]{1,0:T(8,128)(2,1)} copy(bf16[256,2048]{1,0:T(8,128)(2,1)} %get-tuple-element.26) | data formatting | bytes 2097152

commit v6 on v5

--- a/solution.py
+++ b/solution.py
@@ -48,8 +48,9 @@
                xr, xs, w1buf, w2buf, log_s, cand, cands, rk, rks, rt_s, w_s, c64_s,
                p_s, v_s, vt_s, q_s, pick_s, hacc, h_s, zc_s, zs, recv,
                r2_s, gt_s, at_s, a_s, out_s,
-               w1sem, w2sem, xsem, osem, csend, crecv, ksend, krecv, nsem,
-               dsend, drecv, rsend, rrecv):
+               w1sem, w2sem, xsem, osem, lsem, csend, crecv, ksend, krecv, xsend, xfsend, psend, precv, xrecv, xfrecv,
+               zsend, zfsend, osend, zrecv, zfrecv):
+    split = ns1 >= NG and ns2 >= NG
     me = lax.axis_index("ep")
     k = me % 2
     chip = me // 2
@@ -84,23 +85,32 @@
         return xr.at[c, pl.ds(2 * TOK + (2 * n + core) * xb, xb), :]
 
     def x_copy(c):
-        return pltpu.make_async_copy(tok.at[:, pl.ds(c * CW, CW)], xown(c, k), xsem.at[c])
-
-    def p_copy(c, core):
-        return rcopy(xown(c, core), xown(c, core), dsend.at[c * 7 + 6], drecv.at[c * DEV + 6], partner)
-
-    def x_send(c, n):
-        return rcopy(xs.at[c, pl.ds(n * xb, xb), :], xlist(c, n, k), dsend.at[c * 7 + n],
-                     drecv.at[c * DEV + 2 * n + k], far[n])
-
-    def x_fwd(c, n, core):
-        return rcopy(xlist(c, n, core), xlist(c, n, core), dsend.at[c * 7 + 3 + n],
-                     drecv.at[c * DEV + 2 * n + core], partner)
+        return pltpu.make_async_copy(tok.at[:, pl.ds(c * CW, CW)], xown(c, k), xsem)
+
+    def await_bytes(ref, sem):
+        pltpu.make_async_copy(ref, ref, sem).wait()
+
+    def lanes(h):
+        return pl.ds(0, CW) if h is None else pl.ds(h * (CW // 2), CW // 2)
+
+    def p_copy(c):
+        return rcopy(xown(c, k), xown(c, k), psend, precv, partner)
+
+    def x_unit(c, h):
+        return NC if h == 1 else c
+
+    def x_send(c, n, h=None):
+        return rcopy(xs.at[c, pl.ds(n * xb, xb), lanes(h)], xlist(c, n, k).at[:, lanes(h)], xsend,
+                     xrecv.at[x_unit(c, h)], far[n])
+
+    def x_fwd(c, n, h=None):
+        block = xlist(c, n, k).at[:, lanes(h)]
+        return rcopy(block, block, xfsend, xfrecv.at[x_unit(c, h)], partner)
 
     barrier = pltpu.get_barrier_semaphore()
     for j in range(1, DEV):
         pl.semaphore_signal(barrier, inc=1, device_id={"ep": (me + j) % DEV}, device_id_type=MESH)
-    log_copy = pltpu.make_async_copy(logit, log_s, nsem.at[0])
+    log_copy = pltpu.make_async_copy(logit, log_s, lsem)
     log_copy.start()
     for c in range(NC):
         x_copy(c).start()
@@ -115,29 +125,26 @@
     lax.fori_loop(0, 8, next_top, jnp.full((1, ALL_EXP), jnp.inf, F32))
     pl.semaphore_wait(barrier, DEV - 1)
 
-    def c_copy(j, src):
-        return rcopy(cand, cands.at[pl.ds(src * 8, 8), :], csend.at[j], crecv.at[src], (me + j) % DEV)
-
-    def k_copy(j, src):
-        return rcopy(rk, rks.at[pl.ds(src * 8, 8), :], ksend.at[j], krecv.at[src], (me + j) % DEV)
-
+    def c_copy(j):
+        return rcopy(cand, cands.at[pl.ds(me * 8, 8), :], csend, crecv, (me + j) % DEV)
+
+    def k_copy(j):
+        return rcopy(rk, rks.at[pl.ds(me * 8, 8), :], ksend, krecv, (me + j) % DEV)
+
+    seven = cands.at[pl.ds(0, 8 * (DEV - 1)), :]
     for j in range(1, DEV):
-        c_copy(j, me).start()
+        c_copy(j).start()
     cands[pl.ds(me * 8, 8), :] = cand[...]
 
-    def start_own(c, _):
-        x_copy(c).wait()
-        p_copy(c, k).start()
-        return 0
-
-    lax.fori_loop(0, NC, start_own, 0)
+    await_bytes(out_s, xsem)
+    for c in range(NC):
+        p_copy(c).start()
     if nx > 2 * TOK + 6 * xb:
         for c in range(NC):
             xr[c, 2 * TOK + 6 * xb:, :] = jnp.zeros((nx - 2 * TOK - 6 * xb, CW), BF16)
     t0, t1 = iota((TOK, TOK), 0), iota((TOK, TOK), 1)
     tri = onehot(t0 < t1)
-    for j in range(1, DEV):
-        c_copy(j, (me + j) % DEV).wait_recv()
+    await_bytes(seven, crecv)
 
     def next_max(_, m):
         v = cands[...]
@@ -175,9 +182,16 @@
 
     lax.fori_loop(0, 8, top_place, 0)
     for j in range(1, DEV):
-        k_copy(j, me).start()
+        k_copy(j).start()
     rks[pl.ds(me * 8, 8), :] = rk[...]
-    lax.fori_loop(1, NC, compact, 0)
+    lax.fori_loop(1, NC - 1, compact, 0)
+    if split:
+        xs[NC - 1] = dot(w_s[...], xr[NC - 1, pl.ds(k * TOK, TOK), :]).astype(BF16)
+        for h in range(2):
+            for n in (2, 0, 1):
+                x_send(NC - 1, n, h).start()
+    else:
+        compact(NC - 1, 0)
     for i in range(ns1):
         w1_copy(i).start()
     for i in range(ns2):
@@ -203,8 +217,7 @@
     ex = jnp.exp(la - jnp.max(la, axis=0, keepdims=True))
     gt_s[...] = ex / jnp.sum(ex, axis=0, keepdims=True)
 
-    for j in range(1, DEV):
-        k_copy(j, (me + j) % DEV).wait_recv()
+    await_bytes(seven, krecv)
     rv = rks[...]
     src = iota((64, ALL_EXP), 0) >> 3
     exp_chip = iota((64, ALL_EXP), 1) >> 6
@@ -234,33 +247,34 @@
         q_s[n * bound:(n + 1) * bound, :] = onehot(vt_s[0:1, :] == want)
     hacc[...] = jnp.zeros((SLOTS, FF), F32)
 
-    def x_forward(c):
+    def x_forward(c, h=None):
+        await_bytes(xs.at[c, :, lanes(h)], xrecv.at[x_unit(c, h)])
         for n in range(3):
-            x_fwd(c, n, k).wait_recv()
-            x_fwd(c, n, k).start()
-
-    def first_product(c, last):
-        for n in range(3):
-            x_fwd(c, n, 1 - k).wait_recv()
-        p_copy(c, 1 - k).wait_recv()
-        pick_s[...] = dot(p_s[...], xr[c]).astype(BF16)
+            x_fwd(c, n, h).start()
+
+    def first_product(c, last, h=None):
+        cols = lanes(h)
+        await_bytes(xs.at[c, :, cols], xfrecv.at[x_unit(c, h)])
+        pick_s[:, cols] = dot(p_s[...], xr[c, :, cols]).astype(BF16)
 
         def group(g, _):
             i = c * NG + 2 * g
-            w1_copy(i).wait()
-            w1_copy(i + 1).wait()
+            if h != 1:
+                w1_copy(i).wait()
+                w1_copy(i + 1).wait()
             for j in range(2 * GE):
                 rows = pl.ds(g * (2 * GE * CAP) + j * CAP, CAP)
-                v = hacc[rows, :] + dot(pick_s[rows, :], w1buf[(i + j // GE) % ns1, j % GE])
+                v = hacc[rows, :] + dot(pick_s[rows, cols], w1buf[(i + j // GE) % ns1, j % GE, cols, :])
                 if last:
                     h_s[rows, :] = gelu(v).astype(BF16)
                 else:
                     hacc[rows, :] = v
 
-            for n in (i, i + 1):
-                @pl.when(n + ns1 < ITEMS)
-                def _():
-                    w1_copy(n + ns1).start()
+            if h is None:
+                for n in (i, i + 1):
+                    @pl.when(n + ns1 < ITEMS)
+                    def _():
+                        w1_copy(n + ns1).start()
 
             return 0
 
@@ -271,45 +285,74 @@
         first_product(c, False)
         return 0
 
+    await_bytes(out_s, precv)
     x_forward(0)
-    lax.fori_loop(0, NC - 1, chunk, 0)
-    first_product(NC - 1, True)
-
-    def rblk(c, d):
-        return recv.at[c, pl.ds(d * bound, bound), :]
-
-    def z_copy(c, n, dev):
-        src = rblk(c, me) if n == 3 else zs.at[c, pl.ds(n * bound, bound), :]
-        return rcopy(src, rblk(c, me), rsend.at[c * 7 + n], rrecv.at[c * DEV + me], dev)
-
-    def fwd_copy(c, n, block):
-        return rcopy(rblk(c, block), rblk(c, block), rsend.at[c * 7 + 4 + n], rrecv.at[c * DEV + block], partner)
-
-    def second_product(c, _):
+    lax.fori_loop(0, NC - 2, chunk, 0)
+    if split:
+        x_forward(NC - 1, 0)
+        first_product(NC - 2, False)
+        x_forward(NC - 1, 1)
+        first_product(NC - 1, False, 0)
+        first_product(NC - 1, True, 1)
+    else:
+        x_forward(NC - 1)
+        first_product(NC - 2, False)
+        first_product(NC - 1, True)
+
+    def rblk(c, d, h):
+        return recv.at[c, pl.ds(d * bound, bound), lanes(h)]
+
+    def z_unit(c, h):
+        return c if h != 1 else (NC if c == 0 else NC + 1)
+
+    def z_copy(c, n, dev, h=None):
+        block = rblk(c, me, h)
+        if n == 3:
+            return rcopy(block, block, osend, zfrecv.at[c if h is None or c == 0 else z_unit(c, h)], dev)
+        return rcopy(zs.at[c, pl.ds(n * bound, bound), lanes(h)], block, zsend, zrecv.at[z_unit(c, h)], dev)
+
+    def fwd_copy(c, d, h=None):
+        return rcopy(rblk(c, d, h), rblk(c, d, h), zfsend, zfrecv.at[z_unit(c, h)], partner)
+
+    def second_product(c, h=None):
+        cols = lanes(h)
+
         def group(g, _):
             i = c * NG + 2 * g
-            w2_copy(i).wait()
-            w2_copy(i + 1).wait()
+            if h != 1:
+                w2_copy(i).wait()
+                w2_copy(i + 1).wait()
             for j in range(2 * GE):
                 rows = pl.ds(g * (2 * GE * CAP) + j * CAP, CAP)
-                zc_s[rows, :] = dot(h_s[rows, :], w2buf[(i + j // GE) % ns2, j % GE]).astype(BF16)
-
-            for n in (i, i + 1):
-                @pl.when(n + ns2 < ITEMS)
-                def _():
-                    w2_copy(n + ns2).start()
+                zc_s[rows, cols] = dot(h_s[rows, :], w2buf[(i + j // GE) % ns2, j % GE, :, cols]).astype(BF16)
+
+            if h != 0:
+                for n in (i, i + 1):
+                    @pl.when(n + ns2 < ITEMS)
+                    def _():
+                        w2_copy(n + ns2).start()
 
             return 0
 
         lax.fori_loop(0, NG // 2, group, 0)
-        zc = zc_s[...]
-        zs[c] = dot(q_s[:3 * bound, :], zc).astype(BF16)
-        recv[c, pl.ds(me * bound, bound), :] = dot(q_s[3 * bound:, :], zc).astype(BF16)
+        zc = zc_s[:, cols]
+        zs[c, :, cols] = dot(q_s[:3 * bound, :], zc).astype(BF16)
+        recv[c, pl.ds(me * bound, bound), cols] = dot(q_s[3 * bound:, :], zc).astype(BF16)
         for n, dev in ((2, dg), (0, xn), (1, yn), (3, partner)):
-            z_copy(c, n, dev).start()
-        return 0
-
-    lax.fori_loop(0, NC, second_product, 0)
+            z_copy(c, n, dev, h).start()
+
+    def second(c, _):
+        second_product(c)
+        return 0
+
+    if split:
+        second_product(0, 0)
+        second_product(0, 1)
+        lax.fori_loop(1, NC - 1, second, 0)
+        second_product(NC - 1, 0)
+        second_product(NC - 1, 1)
+    else:
+        lax.fori_loop(0, NC, second, 0)
 
     RB = 64
 
@@ -337,58 +380,54 @@
 
     lax.fori_loop(0, DEV * bound // 128, split_a, 0)
 
-    def forward(c):
-        for n, d in enumerate((xn, yn, dg)):
-            fwd_copy(c, n, d).wait_recv()
-            fwd_copy(c, n, d).start()
-
-    def out_copy(c):
-        return pltpu.make_async_copy(out_s.at[c], out.at[:, pl.ds(c * CW, CW)], osem.at[c])
-
-    def combine(c):
-        for d in (partner, xn + other, yn + other, dg + other):
-            fwd_copy(c, 0, d).wait_recv()
-        z = recv[c]
+    def forward(c, h=None):
+        if split and h is None and isinstance(c, int):
+            await_bytes(zs.at[c, :, lanes(0)], zrecv.at[z_unit(c, 0)])
+            await_bytes(zs.at[c, :, lanes(1)], zrecv.at[z_unit(c, 1)])
+        else:
+            await_bytes(zs.at[c, :, lanes(h)], zrecv.at[z_unit(c, h)])
+        for d in far:
+            fwd_copy(c, d, h).start()
+
+    def out_copy(c, h):
+        half = 0 if h is None else h * (CW // 2)
+        return pltpu.make_async_copy(out_s.at[c, :, lanes(h)],
+                                     out.at[:, pl.ds(c * CW + half, CW if h is None else CW // 2)], osem)
+
+    def combine(c, h=None):
+        cols = lanes(h)
+        await_bytes(recv.at[c, pl.ds(0, 4 * bound), cols], zfrecv.at[z_unit(c, h)])
+        z = recv[c, :, cols]
         y = dot(a_s[2], z) + dot(a_s[1], z) + dot(a_s[0], z)
-        out_s[c] = (xr[c, pl.ds(k * TOK, TOK), :].astype(F32) + y).astype(BF16)
-        out_copy(c).start()
-
-    for j in range(1, DEV):
-        c_copy(j, me).wait_send()
-        k_copy(j, me).wait_send()
-
-    def drain_x(c, _):
-        p_copy(c, k).wait_send()
-        for n in range(3):
-            x_send(c, n).wait_send()
-            x_fwd(c, n, k).wait_send()
-        return 0
-
-    lax.fori_loop(0, NC, drain_x, 0)
-
-    def drain_z(c):
-        for n, dev in enumerate((xn, yn, dg, partner)):
-            z_copy(c, n, dev).wait_send()
-        for n, d in enumerate((xn, yn, dg)):
-            fwd_copy(c, n, d).wait_send()
-        out_copy(c).wait()
-
-    forward(0)
+        out_s[c, :, cols] = (xr[c, pl.ds(k * TOK, TOK), cols].astype(F32) + y).astype(BF16)
+        out_copy(c, h).start()
 
     def step(c, _):
         forward(c + 1)
         combine(c)
-
-        @pl.when(c > 0)
-        def _():
-            drain_z(c - 1)
-
-        return 0
-
-    lax.fori_loop(0, NC - 1, step, 0)
-    combine(NC - 1)
-    drain_z(NC - 2)
-    drain_z(NC - 1)
+        return 0
+
+    await_bytes(seven, csend)
+    await_bytes(seven, ksend)
+    await_bytes(out_s, psend)
+    await_bytes(xs, xsend)
+    await_bytes(xs, xfsend)
+    forward(0)
+    lax.fori_loop(0, NC - 2, step, 0)
+    if split:
+        forward(NC - 1, 0)
+        combine(NC - 2)
+        forward(NC - 1, 1)
+        combine(NC - 1, 0)
+        combine(NC - 1, 1)
+    else:
+        forward(NC - 1)
+        combine(NC - 2)
+        combine(NC - 1)
+    await_bytes(zs, zsend)
+    await_bytes(recv.at[:, pl.ds(0, bound), :], osend)
+    await_bytes(zs, zfsend)
+    await_bytes(out_s, osem)
 
 
 def moe_call(xb, bound, ns1, ns2, cid, tok, logit, w1, w2):
@@ -410,8 +449,8 @@
             vm((SLOTS, CW), BF16), vm((SLOTS, FF), F32), vm((SLOTS, FF), BF16), vm((SLOTS, CW), BF16),
             vm((NC, 3 * bound, CW), BF16), vm((NC, DEV * bound, CW), BF16),
             sq, sq, vm((DEV * bound, TOK), F32), vm((3, TOK, DEV * bound), BF16), vm((NC, TOK, CW), BF16),
-            sem((ns1,)), sem((ns2,)), sem((NC,)), sem((NC,)), sem((DEV,)), sem((DEV,)), sem((DEV,)), sem((DEV,)),
-            sem((1,)), sem((NC * 7,)), sem((NC * DEV,)), sem((NC * 7,)), sem((NC * DEV,)),
+            sem((ns1,)), sem((ns2,)), *[sem] * 11, sem((NC + 1,)), sem((NC + 1,)), *[sem] * 3,
+            sem((NC + 2,)), sem((NC + 2,)),
         ],
         compiler_params=pltpu.CompilerParams(collective_id=cid, has_side_effects=True, vmem_limit_bytes=67043328),
         name=f"moe_{bound}",

time: 86.2 us -> 84.2 us (0.977)
  Pallas kernels: 82.9 us -> 81.2 us
    pallas_call x1, Pallas kernels: 82.9 us -> 81.2 us  [moe_call(): pl.pallas_call(functools.partial(moe_kernel, xb, nx, bound, ns1, ns2), ou...]
where the time goes in v6:
time: 84.2 us; the launch traced here: 84.1 us
  Pallas kernels  81.2 us (96%)
  local copies, waits for them, and re-layouts  2.3 us (3%)
    pallas_call x1, Pallas kernels, moe_call(): pl.pallas_call(functools.partial(moe_kernel, xb, nx, bound, ns1, ns2), ou...  81.2 us
    unnamed x1, local copies, waits for them, and re-layouts  2.3 us

profile of v6, /device:TPU:0, one launch (start us, length us, event | category | flops | bytes accessed | tf_op | source)
XLA Modules:
  0.0 84.1 jit_solution(11364576152340097347)
XLA Ops:
  0.0 81.2 %moe_192.1 = (bf16[256,2048]{1,0:T(8,128)(2,1)}, s32[1,1]{1,0:T(1,128)}) custom-call(bf16[256,2048]{1,0:T(8,128)(2,1)} %tok.1, f32[256,256]{1,0:T(8,128)} %logit.1, bf16[32,2048,512]{2,1,0:T(8,128)(2,1)} %w1.1, bf16[32,512,2048]{2,1,0:T(8,128)(2,1)} %w2.1), custom_call_target="tpu_custom_call" | custom-call | tf_op jit(solution)/shard_map/moe_192/pallas_call | solution.py:438
  81.8 2.3 %copy.10 = bf16[256,2048]{1,0:T(8,128)(2,1)} copy(bf16[256,2048]{1,0:T(8,128)(2,1)} %get-tuple-element.26) | data formatting | bytes 2097152
  (1 shorter events, 0.0 us)

commit v7 on v5

v7 whole, which is shorter than its diff:
```python
import functools

import jax
import jax.numpy as jnp
from jax import lax
from jax.experimental import pallas as pl
from jax.experimental.pallas import tpu as pltpu
from jax.sharding import PartitionSpec as P

MESH = pl.DeviceIdType.MESH
F32, BF16 = jnp.float32, jnp.bfloat16
DEV = 8
TOK = 256
D = 2048
FF = 512
EXP = 32
ALL_EXP = EXP * DEV
CAP = 16
SLOTS = EXP * CAP
NC = 8
CW = D // NC
HW = CW // 2


def dot(a, b):
    return jnp.dot(a, b, preferred_element_type=F32)


def iota(shape, dim):
    return lax.broadcasted_iota(jnp.int32, shape, dim)


def gelu(v):
    return 0.5 * v * (1.0 + lax.erf(v * 0.7071067811865476))


def dot_nt(a, b):
    return lax.dot_general(a, b, (((1,), (1,)), ((), ())), preferred_element_type=F32)


def onehot(cond):
    return jnp.where(cond, 1.0, 0.0).astype(BF16)


def moe_kernel(xb, nx, bound, ge, ns1, ns2, nz, tok, logit, w1, w2, out, flag_out,
               xr, xs, w1buf, w2buf, log_s, cand, cands, rk, rks, rt_s, w_s, c64_s,
               p_s, v_s, vt_s, q_s, pick_s, hacc, h_s, zc_s, zq, zin, zown, zs, recv,
               r2_s, gt_s, at_s, a_s, out_s,
               w1sem, w2sem, xsem, osem, lsem, csend, crecv, ksend, krecv, xsend, xfsend, psend, precv, xrecv, xfrecv,
               zsend, zfsend, zrecv, zfrecv, qsend, qrecv):
    groups = EXP // ge
    items = NC * groups
    rows_in = recv.shape[1]
    me = lax.axis_index("ep")
    k = me % 2
    chip = me // 2
    cx = chip % 2
    cy = chip // 2
    dx = 2 - 4 * cx
    dy = 4 - 8 * cy
    other = 1 - 2 * k
    partner = me + other
    xn, yn, dg = me + dx, me + dy, me + dx + dy
    far = (xn, yn, dg)
    neg = jnp.float32(-jnp.inf)

    def rcopy(src, dst, ss, rs, dev):
        return pltpu.make_async_remote_copy(src_ref=src, dst_ref=dst, send_sem=ss, recv_sem=rs,
                                            device_id={"ep": dev}, device_id_type=MESH)

    def w1_copy(i):
        s = i % ns1
        return pltpu.make_async_copy(
            w1.at[pl.ds((i % groups) * ge, ge), pl.ds((i // groups) * CW, CW), :], w1buf.at[s], w1sem.at[s])

    def w2_copy(i):
        s = i % ns2
        return pltpu.make_async_copy(
            w2.at[pl.ds((i % groups) * ge, ge), :, pl.ds((i // groups) * CW, CW)], w2buf.at[s], w2sem.at[s])

    def xown(c, core):
        return xr.at[c, pl.ds(core * TOK, TOK), :]

    def xlist(c, n, core):
        return xr.at[c, pl.ds(2 * TOK + (2 * n + core) * xb, xb), :]

    def x_copy(c):
        return pltpu.make_async_copy(tok.at[:, pl.ds(c * CW, CW)], xown(c, k), xsem)

    def await_bytes(ref, sem):
        pltpu.make_async_copy(ref, ref, sem).wait()

    def p_copy(c):
        return rcopy(xown(c, k), xown(c, k), psend, precv, partner)

    def x_send(c, n):
        return rcopy(xs.at[c, pl.ds(n * xb, xb), :], xlist(c, n, k), xsend, xrecv.at[c], far[n])

    def x_fwd(c, n):
        return rcopy(xlist(c, n, k), xlist(c, n, k), xfsend, xfrecv.at[c], partner)

    log_copy = pltpu.make_async_copy(logit, log_s, lsem)
    log_copy.start()
    barrier = pltpu.get_barrier_semaphore()
    for j in range(1, DEV):
        pl.semaphore_signal(barrier, inc=1, device_id={"ep": (me + j) % DEV}, device_id_type=MESH)
    for c in range(NC):
        x_copy(c).start()
    log_copy.wait()

    def next_top(n, m):
        v = log_s[...]
        m = jnp.max(jnp.where(v < m, v, neg), axis=0, keepdims=True)
        cand[pl.ds(n, 1), :] = m
        return m

    lax.fori_loop(0, 8, next_top, jnp.full((1, ALL_EXP), jnp.inf, F32))
    pl.semaphore_wait(barrier, DEV - 1)

    def c_copy(j):
        return rcopy(cand, cands.at[pl.ds(me * 8, 8), :], csend, crecv, (me + j) % DEV)

    def k_copy(j):
        return rcopy(rk, rks.at[pl.ds(me * 8, 8), :], ksend, krecv, (me + j) % DEV)

    seven = cands.at[pl.ds(0, 8 * (DEV - 1)), :]
    for j in range(1, DEV):
        c_copy(j).start()
    cands[pl.ds(me * 8, 8), :] = cand[...]

    await_bytes(out_s, xsem)
    for c in range(NC):
        p_copy(c).start()
    if rows_in > 4 * bound:
        for c in range(NC):
            recv[c, 4 * bound:, :] = jnp.zeros((rows_in - 4 * bound, CW), BF16)
        at_s[4 * bound:, :] = jnp.zeros((rows_in - 4 * bound, TOK), F32)
    if nx > 2 * TOK + 6 * xb:
        for c in range(NC):
            xr[c, 2 * TOK + 6 * xb:, :] = jnp.zeros((nx - 2 * TOK - 6 * xb, CW), BF16)
    t0, t1 = iota((TOK, TOK), 0), iota((TOK, TOK), 1)
    tri = onehot(t0 < t1)
    await_bytes(seven, crecv)

    def next_max(_, m):
        v = cands[...]
        return jnp.max(jnp.where(v < m, v, neg), axis=0, keepdims=True)

    thr = lax.fori_loop(0, CAP, next_max, jnp.full((1, ALL_EXP), jnp.inf, F32))

    mo = onehot(log_s[...] >= thr)
    of_chip = onehot((iota((16, ALL_EXP), 1) >> 6) == iota((16, ALL_EXP), 0))
    used = dot_nt(of_chip, mo) > 0.5
    rt_s[...] = jnp.where(used, dot(onehot(used), tri), -1.0)
    xio = iota((xb, TOK), 0).astype(F32)
    for n in range(3):
        w_s[n * xb:(n + 1) * xb, :] = onehot(rt_s[pl.ds(far[n] // 2, 1), :] == xio)

    def compact(c, _):
        xs[c] = dot(w_s[...], xr[c, pl.ds(k * TOK, TOK), :]).astype(BF16)
        for n in (2, 0, 1):
            x_send(c, n).start()
        return 0

    compact(0, 0)

    of_chip2 = onehot((iota((ALL_EXP, 128), 0) >> 6) == iota((ALL_EXP, 128), 1))
    used2 = onehot(dot(mo, of_chip2) > 0.5)
    place = dot(onehot(t1 < t0), used2)
    place = jnp.where(iota((TOK, 128), 1) == chip, iota((TOK, 128), 0).astype(F32), place)
    place = dot_nt(place.astype(BF16), of_chip2)
    c64_s[...] = place

    def top_place(n, _):
        hit = log_s[...] == cand[pl.ds(n, 1), :]
        rk[pl.ds(n, 1), :] = jnp.max(jnp.where(hit, c64_s[...], -1.0), axis=0, keepdims=True)
        return 0

    lax.fori_loop(0, 8, top_place, 0)
    for j in range(1, DEV):
        k_copy(j).start()
    rks[pl.ds(me * 8, 8), :] = rk[...]
    lax.fori_loop(1, NC, compact, 0)
    for i in range(ns1):
        w1_copy(i).start()
    for i in range(ns2):
        w2_copy(i).start()

    cv = cands[...]
    sel = cv >= thr
    so = onehot(sel)
    j0, j1 = iota((64, 64), 0), iota((64, 64), 1)
    slot = dot(onehot(j1 < j0), so)
    inside = dot(onehot((j1 < j0) & ((j1 >> 4) == (j0 >> 4))), so)
    num = dot(onehot((j1 >> 4) == (j0 >> 4)), so)
    base = dot(num.astype(BF16), onehot((t0 < t1) & ((t0 >> 6) == (t1 >> 6))))
    rank = base + inside
    over = jnp.max(jnp.max(base + num, axis=0, keepdims=True), axis=1, keepdims=True) > bound
    c64_s[:64, :] = jnp.where(sel, rank, -1.0)

    pair = jnp.full((TOK, ALL_EXP), -1.0, F32)
    for n in range(8):
        pair = jnp.where(log_s[...] == cand[n:n + 1, :], c64_s[pl.ds(me * 8 + n, 1), :], pair)
    r2_s[...] = pair.T
    la = log_s[...].T
    ex = jnp.exp(la - jnp.max(la, axis=0, keepdims=True))
    gt_s[...] = ex / jnp.sum(ex, axis=0, keepdims=True)

    await_bytes(seven, krecv)
    rv = rks[...]
    src = iota((64, ALL_EXP), 0) >> 3
    exp_chip = iota((64, ALL_EXP), 1) >> 6
    wide = jnp.max(jnp.max(jnp.where(sel & ((src >> 1) != exp_chip), rv, -1.0), axis=0, keepdims=True),
                   axis=1, keepdims=True) >= xb
    flag_out[0, 0] = jnp.max(jnp.where(over | wide, 1.0, 0.0)).astype(jnp.int32)
    rel = (src >> 1) ^ chip
    start = jnp.where(rel == 0, (src & 1) * TOK, 2 * TOK + (2 * (rel - 1) + (src & 1)) * xb).astype(F32)
    pos = start + rv + 1.0
    code = ((src >> 1) * 1024).astype(F32) + rank + 1.0
    pos_rows, code_rows = [], []
    for i in range(CAP):
        hit = sel & (slot == i)
        pos_rows.append(jnp.sum(jnp.where(hit, pos, 0.0), axis=0, keepdims=True))
        code_rows.append(jnp.sum(jnp.where(hit, code, 0.0), axis=0, keepdims=True))
    turn = ALL_EXP - me * EXP
    pos = pltpu.roll(jnp.concatenate(pos_rows, axis=0), turn, 1)
    code = pltpu.roll(jnp.concatenate(code_rows, axis=0), turn, 1)
    pio = iota((CAP, nx), 1).astype(F32) + 1.0
    for e in range(EXP):
        p_s[e * CAP:(e + 1) * CAP, :] = onehot(pos[:, e:e + 1] == pio)
        v_s[e * CAP:(e + 1) * CAP, :] = jnp.broadcast_to(code[:, e:e + 1], (CAP, 128))
    vt_s[...] = v_s[...].T[:8, :]
    rio = iota((bound, SLOTS), 0)
    for n, d in enumerate((xn, yn, dg, me)):
        want = (rio + ((d // 2) * 1024 + 1)).astype(F32)
        q_s[n * bound:(n + 1) * bound, :] = onehot(vt_s[0:1, :] == want)
    hacc[...] = jnp.zeros((SLOTS, FF), F32)

    def x_forward(c):
        await_bytes(xs.at[c], xrecv.at[c])
        for n in range(3):
            x_fwd(c, n).start()

    def first_product(c, last):
        await_bytes(xs.at[c], xfrecv.at[c])
        pick_s[...] = dot(p_s[...], xr[c]).astype(BF16)

        def group(g, _):
            i = c * groups + 2 * g
            w1_copy(i).wait()
            w1_copy(i + 1).wait()
            for j in range(2 * ge):
                rows = pl.ds(g * (2 * ge * CAP) + j * CAP, CAP)
                v = hacc[rows, :] + dot(pick_s[rows, :], w1buf[(i + j // ge) % ns1, j % ge])
                if last:
                    h_s[rows, :] = gelu(v).astype(BF16)
                else:
                    hacc[rows, :] = v

            for n in (i, i + 1):
                @pl.when(n + ns1 < items)
                def _():
                    w1_copy(n + ns1).start()

            return 0

        lax.fori_loop(0, groups // 2, group, 0)

    def chunk(c, _):
        x_forward(c + 1)
        first_product(c, False)
        return 0

    await_bytes(out_s, precv)
    x_forward(0)
    lax.fori_loop(0, NC - 1, chunk, 0)
    first_product(NC - 1, True)

    RB = 64 if bound % 64 == 0 else 48

    def build_a(n, _):
        o = n // (bound // RB)
        r0 = (n % (bound // RB)) * RB
        rio2 = (iota((RB, TOK), 0) + r0).astype(F32)

        def one(e, acc):
            row = pl.ds(o * 2 * EXP + e, 1)
            return jnp.where(r2_s[row, :] == rio2, gt_s[row, :], acc)

        at_s[pl.ds(o * bound + r0, RB), :] = lax.fori_loop(0, 2 * EXP, one, jnp.zeros((RB, TOK), F32), unroll=8)
        return 0

    blocks = 4 * (bound // RB)
    turns = NC - 1 if blocks % (NC - 1) == 0 else NC
    per = blocks // turns

    mine = pl.ds(pl.multiple_of(k * HW, HW), HW)
    theirs = pl.ds(pl.multiple_of((1 - k) * HW, HW), HW)

    def rblk(c, d):
        return recv.at[c, pl.ds((d // 2) * bound, bound), mine]

    def q_copies(s):
        return (rcopy(zq.at[s, pl.ds(0, 3 * bound), theirs], zin.at[s], qsend.at[s], qrecv.at[s], partner),
                rcopy(zq.at[s, pl.ds(3 * bound, bound), :], zown.at[s], qsend.at[s], qrecv.at[s], partner))

    def z_copy(c, n, dev):
        return rcopy(zs.at[c % nz, pl.ds(n * bound, bound), :], rblk(c, me), zsend.at[c % nz], zrecv.at[c], dev)

    def fwd_copy(c, d):
        return rcopy(rblk(c, d), rblk(c, d), zfsend, zfrecv.at[c], partner)

    def q_bytes(s):
        return zq.at[s, pl.ds(0, 5 * bound // 2), :]

    def merge(c):
        s = c % 2
        await_bytes(q_bytes(s), qrecv.at[s])
        if nz < NC:
            @pl.when(c >= nz)
            def _():
                await_bytes(zs.at[c % nz], zsend.at[c % nz])
        zs[c % nz] = zq[s, :3 * bound, mine] + zin[s]
        recv[c, pl.ds(chip * bound, bound), :] = zq[s, 3 * bound:, :] + zown[s]
        for n, dev in ((2, dg), (0, xn), (1, yn)):
            z_copy(c, n, dev).start()

    def forward(c):
        await_bytes(zs.at[0], zrecv.at[c])
        for d in far:
            fwd_copy(c, d).start()

    def second_product(c, _):
        def group(g, _):
            i = c * groups + 2 * g
            w2_copy(i).wait()
            w2_copy(i + 1).wait()
            for j in range(2 * ge):
                rows = pl.ds(g * (2 * ge * CAP) + j * CAP, CAP)
                zc_s[rows, :] = dot(h_s[rows, :], w2buf[(i + j // ge) % ns2, j % ge]).astype(BF16)

            for n in (i, i + 1):
                @pl.when(n + ns2 < items)
                def _():
                    w2_copy(n + ns2).start()

            return 0

        lax.fori_loop(0, groups // 2, group, 0)
        @pl.when(c > 1)
        def _():
            await_bytes(q_bytes(c % 2), qsend.at[c % 2])

        zq[c % 2] = dot(q_s[...], zc_s[...]).astype(BF16)
        for copy in q_copies(c % 2):
            copy.start()

        @pl.when(c < turns)
        def _():
            lax.fori_loop(c * per, (c + 1) * per, build_a, 0)

        merge(c)

        @pl.when(c > 3)
        def _():
            forward(c - 4)

        return 0

    lax.fori_loop(0, NC, second_product, 0)
    def cut_a(j, _):
        a = at_s[pl.ds(j * 128, 128), :].T
        for n in range(3):
            part = a.astype(BF16)
            a_s[n, :, pl.ds(j * 128, 128)] = part
            a = a - part.astype(F32)
        return 0

    lax.fori_loop(0, rows_in // 128, cut_a, 0)

    def out_copy(c):
        return pltpu.make_async_copy(out_s.at[c], out.at[:, pl.ds(c * CW, CW)], osem)

    def combine(c):
        recv_half = recv.at[c, pl.ds(0, 3 * bound), pl.ds(0, HW)]
        await_bytes(recv_half, zfrecv.at[c])
        z = recv[c]
        y = dot(a_s[2], z) + dot(a_s[1], z) + dot(a_s[0], z)
        out_s[c] = (xr[c, pl.ds(k * TOK, TOK), :].astype(F32) + y).astype(BF16)
        out_copy(c).start()

    def step(c, _):
        for at, chunk_in in ((1, 5), (6, 6), (6, 7)):
            @pl.when(c == at)
            def _():
                forward(chunk_in)

        combine(c)
        return 0

    await_bytes(seven, csend)
    await_bytes(seven, ksend)
    await_bytes(out_s, psend)
    await_bytes(xs, xsend)
    await_bytes(xs, xfsend)
    forward(4)
    lax.fori_loop(0, NC, step, 0)
    for s in range(2):
        await_bytes(q_bytes(s), qsend.at[s])
    for s in range(nz):
        await_bytes(zs.at[s], zsend.at[s])
    await_bytes(recv.at[:, pl.ds(0, 3 * bound), pl.ds(0, HW)], zfsend)
    await_bytes(out_s, osem)


def moe_call(xb, bound, ge, ns1, ns2, nz, cid, tok, logit, w1, w2):
    nx = -(-(2 * TOK + 6 * xb) // 128) * 128
    rows_in = -(-4 * bound // 128) * 128
    vm = pltpu.VMEM
    sem = pltpu.SemaphoreType.DMA
    sq = vm((ALL_EXP, TOK), F32)
    return pl.pallas_call(
        functools.partial(moe_kernel, xb, nx, bound, ge, ns1, ns2, nz),
        out_shape=(jax.ShapeDtypeStruct((TOK, D), BF16), jax.ShapeDtypeStruct((1, 1), jnp.int32)),
        in_specs=[pl.BlockSpec(memory_space=pl.ANY)] * 4,
        out_specs=(pl.BlockSpec(memory_space=pl.ANY), pl.BlockSpec(memory_space=pltpu.SMEM)),
        scratch_shapes=[
            vm((NC, nx, CW), BF16), vm((NC, 3 * xb, CW), BF16),
            vm((ns1, ge, CW, FF), BF16), vm((ns2, ge, FF, CW), BF16),
            sq, vm((8, ALL_EXP), F32), vm((64, ALL_EXP), F32), vm((8, ALL_EXP), F32), vm((64, ALL_EXP), F32),
            vm((16, TOK), F32), vm((3 * xb, TOK), BF16), sq,
            vm((SLOTS, nx), BF16), vm((SLOTS, 128), F32), vm((8, SLOTS), F32), vm((4 * bound, SLOTS), BF16),
            vm((SLOTS, CW), BF16), vm((SLOTS, FF), F32), vm((SLOTS, FF), BF16), vm((SLOTS, CW), BF16),
            vm((2, 4 * bound, CW), BF16), vm((2, 3 * bound, HW), BF16), vm((2, bound, CW), BF16),
            vm((nz, 3 * bound, HW), BF16), vm((NC, rows_in, CW), BF16),
            sq, sq, vm((rows_in, TOK), F32), vm((3, TOK, rows_in), BF16), vm((NC, TOK, CW), BF16),
            sem((ns1,)), sem((ns2,)), *[sem] * 11, sem((NC,)), sem((NC,)),
            sem((nz,)), sem, sem((NC,)), sem((NC,)), sem((2,)), sem((2,)),
        ],
        compiler_params=pltpu.CompilerParams(collective_id=cid, has_side_effects=True, vmem_limit_bytes=67043328),
        name=f"moe_{bound}",
    )(tok, logit, w1, w2)


def solution(mesh):
    row_spec = P(("dp", "ep"), None)
    expert_spec = P("ep", None, None)

    def device_step(tok, logit, w1, w2):
        out, flag = moe_call(144, 336, 8, 8, 8, NC, 0, tok, logit, w1, w2)
        return lax.switch(flag[0, 0], (lambda: out, lambda: moe_call(TOK, 1024, 2, 2, 2, 2, 1, tok, logit, w1, w2)[0]))

    return jax.shard_map(device_step, mesh=mesh, in_specs=(row_spec, row_spec, expert_spec, expert_spec),
                         out_specs=row_spec, check_vma=False)
```

time: 86.2 us -> 81.9 us (0.950)
  Pallas kernels: 82.9 us -> 78.6 us
    pallas_call x1, Pallas kernels: 82.9 us -> 78.6 us  [moe_call(): pl.pallas_call(functools.partial(moe_kernel, xb, nx, bound, ge, ns1, ns2,...]
where the time goes in v7:
time: 81.9 us; the launch traced here: 81.7 us
  Pallas kernels  78.6 us (96%)
  local copies, waits for them, and re-layouts  2.3 us (3%)
    pallas_call x1, Pallas kernels, moe_call(): pl.pallas_call(functools.partial(moe_kernel, xb, nx, bound, ge, ns1, ns2,...  78.6 us
    unnamed x1, local copies, waits for them, and re-layouts  2.3 us

profile of v7, /device:TPU:0, one launch (start us, length us, event | category | flops | bytes accessed | tf_op | source)
XLA Modules:
  0.0 81.7 jit_solution(6572800701768993700)
XLA Ops:
  0.0 78.6 %moe_336.1 = (bf16[256,2048]{1,0:T(8,128)(2,1)}, s32[1,1]{1,0:T(1,128)}) custom-call(bf16[256,2048]{1,0:T(8,128)(2,1)} %tok.1, f32[256,256]{1,0:T(8,128)} %logit.1, bf16[32,2048,512]{2,1,0:T(8,128)(2,1)} %w1.1, bf16[32,512,2048]{2,1,0:T(8,128)(2,1)} %w2.1), custom_call_target="tpu_custom_call" | custom-call | tf_op jit(solution)/shard_map/moe_336/pallas_call | solution.py:422
  79.2 0.2 conditional.1
  79.4 2.3 %copy.10 = bf16[256,2048]{1,0:T(8,128)(2,1)} copy(bf16[256,2048]{1,0:T(8,128)(2,1)} %get-tuple-element.26) | data formatting | bytes 2097152

commit v8 on v7

--- a/solution.py
+++ b/solution.py
@@ -42,15 +42,16 @@
     return jnp.where(cond, 1.0, 0.0).astype(BF16)
 
 
-def moe_kernel(xb, nx, bound, ge, ns1, ns2, nz, tok, logit, w1, w2, out, flag_out,
-               xr, xs, w1buf, w2buf, log_s, cand, cands, rk, rks, rt_s, w_s, c64_s,
-               p_s, v_s, vt_s, q_s, pick_s, hacc, h_s, zc_s, zq, zin, zown, zs, recv,
+def moe_kernel(xb, nx, bound, ge, ns1, ns2, nz, lag, tok, logit, w1, w2, out, flag_out,
+               xo, xl, xq, xin, xs, plog, w1buf, w2buf, log_s, cand, cands, rk, rks, rt_s, w_s, c64_s,
+               p_s, v_s, vt_s, q_s, pick_s, own_s, hacc, h_s, zc_s, zq, zin, zown, zs, recv,
                r2_s, gt_s, at_s, a_s, out_s,
                w1sem, w2sem, xsem, osem, lsem, csend, crecv, ksend, krecv, xsend, xfsend, psend, precv, xrecv, xfrecv,
-               zsend, zfsend, zrecv, zfrecv, qsend, qrecv):
+               zsend, zfsend, zrecv, zfrecv, qsend, qrecv, xqsend, xqrecv, gsend, grecv):
     groups = EXP // ge
     items = NC * groups
-    rows_in = recv.shape[1]
+    rows_in = recv.shape[2]
+    ahead_of = own_s.shape[0] == NC
     me = lax.axis_index("ep")
     k = me % 2
     chip = me // 2
@@ -79,10 +80,7 @@
             w2.at[pl.ds((i % groups) * ge, ge), :, pl.ds((i // groups) * CW, CW)], w2buf.at[s], w2sem.at[s])
 
     def xown(c, core):
-        return xr.at[c, pl.ds(core * TOK, TOK), :]
-
-    def xlist(c, n, core):
-        return xr.at[c, pl.ds(2 * TOK + (2 * n + core) * xb, xb), :]
+        return xo.at[c, pl.ds(core * TOK, TOK), :]
 
     def x_copy(c):
         return pltpu.make_async_copy(tok.at[:, pl.ds(c * CW, CW)], xown(c, k), xsem)
@@ -94,10 +92,15 @@
         return rcopy(xown(c, k), xown(c, k), psend, precv, partner)
 
     def x_send(c, n):
-        return rcopy(xs.at[c, pl.ds(n * xb, xb), :], xlist(c, n, k), xsend, xrecv.at[c], far[n])
-
-    def x_fwd(c, n):
-        return rcopy(xlist(c, n, k), xlist(c, n, k), xfsend, xfrecv.at[c], partner)
+        part = pl.ds(n * xb, xb)
+        s = c % nz
+        return rcopy(xs.at[s, part, :], xl.at[c, k, part, :], xsend.at[s], xrecv.at[c], far[n])
+
+    def x_fwd(c):
+        return rcopy(xl.at[c, k], xl.at[c, k], xfsend, xfrecv.at[c], partner)
+
+    def x_swap(s):
+        return rcopy(xq.at[s, 1 - k], xin.at[s], xqsend.at[s], xqrecv.at[s], partner)
 
     log_copy = pltpu.make_async_copy(logit, log_s, lsem)
     log_copy.start()
@@ -123,9 +126,11 @@
     def k_copy(j):
         return rcopy(rk, rks.at[pl.ds(me * 8, 8), :], ksend, krecv, (me + j) % DEV)
 
+    log_swap = rcopy(log_s, plog, gsend, grecv, partner)
     seven = cands.at[pl.ds(0, 8 * (DEV - 1)), :]
     for j in range(1, DEV):
         c_copy(j).start()
+    log_swap.start()
     cands[pl.ds(me * 8, 8), :] = cand[...]
 
     await_bytes(out_s, xsem)
@@ -133,14 +138,16 @@
         p_copy(c).start()
     if rows_in > 4 * bound:
         for c in range(NC):
-            recv[c, 4 * bound:, :] = jnp.zeros((rows_in - 4 * bound, CW), BF16)
+            recv[c, :, 4 * bound:, :] = jnp.zeros((2, rows_in - 4 * bound, HW), BF16)
         at_s[4 * bound:, :] = jnp.zeros((rows_in - 4 * bound, TOK), F32)
-    if nx > 2 * TOK + 6 * xb:
-        for c in range(NC):
-            xr[c, 2 * TOK + 6 * xb:, :] = jnp.zeros((nx - 2 * TOK - 6 * xb, CW), BF16)
+    for i in range(ns1):
+        w1_copy(i).start()
+    for i in range(ns2):
+        w2_copy(i).start()
     t0, t1 = iota((TOK, TOK), 0), iota((TOK, TOK), 1)
     tri = onehot(t0 < t1)
     await_bytes(seven, crecv)
+    log_swap.wait_recv()
 
     def next_max(_, m):
         v = cands[...]
@@ -148,28 +155,51 @@
 
     thr = lax.fori_loop(0, CAP, next_max, jnp.full((1, ALL_EXP), jnp.inf, F32))
 
+    core = k.astype(F32)
     mo = onehot(log_s[...] >= thr)
+    mp = onehot(plog[...] >= thr)
     of_chip = onehot((iota((16, ALL_EXP), 1) >> 6) == iota((16, ALL_EXP), 0))
     used = dot_nt(of_chip, mo) > 0.5
-    rt_s[...] = jnp.where(used, dot(onehot(used), tri), -1.0)
+    ahead = core * jnp.sum(jnp.where(dot_nt(of_chip, mp) > 0.5, 1.0, 0.0), axis=1, keepdims=True)
+    rt_s[...] = jnp.where(used, dot(onehot(used), tri) + ahead, -1.0)
     xio = iota((xb, TOK), 0).astype(F32)
     for n in range(3):
         w_s[n * xb:(n + 1) * xb, :] = onehot(rt_s[pl.ds(far[n] // 2, 1), :] == xio)
 
-    def compact(c, _):
-        xs[c] = dot(w_s[...], xr[c, pl.ds(k * TOK, TOK), :]).astype(BF16)
+    nq = 2 * lag
+
+    def compact(c):
+        s = c % nq
+        new = dot(w_s[...], xo[c, pl.ds(k * TOK, TOK), :]).astype(BF16)
+        xq[s, 0] = new[:, :HW]
+        xq[s, 1] = new[:, HW:]
+        x_swap(s).start()
+
+    def x_merge(c):
+        s = c % nq
+        await_bytes(xin.at[s], xqrecv.at[s])
+        if nz < NC and isinstance(c, int):
+            await_bytes(xs.at[c % nz], xsend.at[c % nz])
+        elif nz < NC:
+            @pl.when(c >= nz)
+            def _():
+                await_bytes(xs.at[c % nz], xsend.at[c % nz])
+        xs[c % nz] = xq[s, k] + xin[s]
         for n in (2, 0, 1):
             x_send(c, n).start()
-        return 0
-
-    compact(0, 0)
+
+    for c in range(lag):
+        compact(c)
 
     of_chip2 = onehot((iota((ALL_EXP, 128), 0) >> 6) == iota((ALL_EXP, 128), 1))
     used2 = onehot(dot(mo, of_chip2) > 0.5)
     place = dot(onehot(t1 < t0), used2)
     place = jnp.where(iota((TOK, 128), 1) == chip, iota((TOK, 128), 0).astype(F32), place)
-    place = dot_nt(place.astype(BF16), of_chip2)
-    c64_s[...] = place
+    used_p = jnp.where(dot(mp, of_chip2) > 0.5, 1.0, 0.0)
+    shift = core * jnp.sum(used_p, axis=0, keepdims=True)
+    shift = jnp.broadcast_to(jnp.where(iota((1, 128), 1) == chip, 0.0, shift), (8, 128))
+    shift = dot_nt(shift.astype(BF16), of_chip2)
+    c64_s[...] = dot_nt(place.astype(BF16), of_chip2) + shift[:1, :]
 
     def top_place(n, _):
         hit = log_s[...] == cand[pl.ds(n, 1), :]
@@ -180,11 +210,19 @@
     for j in range(1, DEV):
         k_copy(j).start()
     rks[pl.ds(me * 8, 8), :] = rk[...]
-    lax.fori_loop(1, NC, compact, 0)
-    for i in range(ns1):
-        w1_copy(i).start()
-    for i in range(ns2):
-        w2_copy(i).start()
+    def exchange(c, _):
+        x_merge(c - lag)
+
+        @pl.when(c >= nq)
+        def _():
+            await_bytes(xin.at[c % nq], xqsend.at[c % nq])
+
+        compact(c)
+        return 0
+
+    lax.fori_loop(lag, NC, exchange, 0)
+    for c in range(NC - lag, NC):
+        x_merge(c)
 
     cv = cands[...]
     sel = cv >= thr
@@ -214,7 +252,7 @@
                    axis=1, keepdims=True) >= xb
     flag_out[0, 0] = jnp.max(jnp.where(over | wide, 1.0, 0.0)).astype(jnp.int32)
     rel = (src >> 1) ^ chip
-    start = jnp.where(rel == 0, (src & 1) * TOK, 2 * TOK + (2 * (rel - 1) + (src & 1)) * xb).astype(F32)
+    start = jnp.where(rel == 0, (src & 1) * TOK, 2 * TOK + (rel - 1) * xb).astype(F32)
     pos = start + rv + 1.0
     code = ((src >> 1) * 1024).astype(F32) + rank + 1.0
     pos_rows, code_rows = [], []
@@ -237,13 +275,14 @@
     hacc[...] = jnp.zeros((SLOTS, FF), F32)
 
     def x_forward(c):
-        await_bytes(xs.at[c], xrecv.at[c])
-        for n in range(3):
-            x_fwd(c, n).start()
+        await_bytes(xs.at[0], xrecv.at[c])
+        x_fwd(c).start()
 
     def first_product(c, last):
-        await_bytes(xs.at[c], xfrecv.at[c])
-        pick_s[...] = dot(p_s[...], xr[c]).astype(BF16)
+        await_bytes(xs.at[0], xfrecv.at[c])
+        lists = jnp.concatenate([xl[c, 0], xl[c, 1]], axis=1)
+        near = own_s[c] if ahead_of else dot(p_s[:, :2 * TOK], xo[c])
+        pick_s[...] = (near + dot(p_s[:, 2 * TOK:], lists)).astype(BF16)
 
         def group(g, _):
             i = c * groups + 2 * g
@@ -273,6 +312,13 @@
 
     await_bytes(out_s, precv)
     x_forward(0)
+
+    def pick_own(c, _):
+        own_s[c] = dot(p_s[:, :2 * TOK], xo[c]).astype(BF16)
+        return 0
+
+    if ahead_of:
+        lax.fori_loop(0, NC, pick_own, 0)
     lax.fori_loop(0, NC - 1, chunk, 0)
     first_product(NC - 1, True)
 
@@ -291,18 +337,14 @@
         return 0
 
     blocks = 4 * (bound // RB)
-    turns = NC - 1 if blocks % (NC - 1) == 0 else NC
-    per = blocks // turns
-
-    mine = pl.ds(pl.multiple_of(k * HW, HW), HW)
-    theirs = pl.ds(pl.multiple_of((1 - k) * HW, HW), HW)
+    per = blocks // NC + (blocks % NC > 0)
 
     def rblk(c, d):
-        return recv.at[c, pl.ds((d // 2) * bound, bound), mine]
+        return recv.at[c, k, pl.ds((d // 2) * bound, bound), :]
 
     def q_copies(s):
-        return (rcopy(zq.at[s, pl.ds(0, 3 * bound), theirs], zin.at[s], qsend.at[s], qrecv.at[s], partner),
-                rcopy(zq.at[s, pl.ds(3 * bound, bound), :], zown.at[s], qsend.at[s], qrecv.at[s], partner))
+        return (rcopy(zq.at[s, 1 - k], zin.at[s], qsend.at[s], qrecv.at[s], partner),
+                rcopy(zq.at[s, k, pl.ds(3 * bound, bound), :], zown.at[s], qsend.at[s], qrecv.at[s], partner))
 
     def z_copy(c, n, dev):
         return rcopy(zs.at[c % nz, pl.ds(n * bound, bound), :], rblk(c, me), zsend.at[c % nz], zrecv.at[c], dev)
@@ -311,7 +353,7 @@
         return rcopy(rblk(c, d), rblk(c, d), zfsend, zfrecv.at[c], partner)
 
     def q_bytes(s):
-        return zq.at[s, pl.ds(0, 5 * bound // 2), :]
+        return zq.at[s, :, pl.ds(0, 5 * bound // 2), :]
 
     def merge(c):
         s = c % 2
@@ -320,8 +362,10 @@
             @pl.when(c >= nz)
             def _():
                 await_bytes(zs.at[c % nz], zsend.at[c % nz])
-        zs[c % nz] = zq[s, :3 * bound, mine] + zin[s]
-        recv[c, pl.ds(chip * bound, bound), :] = zq[s, 3 * bound:, :] + zown[s]
+        zs[c % nz] = zq[s, k, :3 * bound, :] + zin[s, :3 * bound, :]
+        home = pl.ds(chip * bound, bound)
+        recv[c, k, home, :] = zq[s, k, 3 * bound:, :] + zin[s, 3 * bound:, :]
+        recv[c, 1 - k, home, :] = zq[s, 1 - k, 3 * bound:, :] + zown[s]
         for n, dev in ((2, dg), (0, xn), (1, yn)):
             z_copy(c, n, dev).start()
 
@@ -349,17 +393,22 @@
         lax.fori_loop(0, groups // 2, group, 0)
         @pl.when(c > 1)
         def _():
+            merge(c - 1)
             await_bytes(q_bytes(c % 2), qsend.at[c % 2])
 
-        zq[c % 2] = dot(q_s[...], zc_s[...]).astype(BF16)
+        zq_new = dot(q_s[...], zc_s[...]).astype(BF16)
+        zq[c % 2, 0] = zq_new[:, :HW]
+        zq[c % 2, 1] = zq_new[:, HW:]
         for copy in q_copies(c % 2):
             copy.start()
 
-        @pl.when(c < turns)
+        @pl.when(c == 0)
         def _():
-            lax.fori_loop(c * per, (c + 1) * per, build_a, 0)
-
-        merge(c)
+            merge(0)
+
+        @pl.when(c > 1)
+        def _():
+            lax.fori_loop((c - 2) * per, (c - 1) * per, build_a, 0)
 
         @pl.when(c > 3)
         def _():
@@ -368,6 +417,8 @@
         return 0
 
     lax.fori_loop(0, NC, second_product, 0)
+    merge(NC - 1)
+    lax.fori_loop((NC - 2) * per, blocks, build_a, 0)
     def cut_a(j, _):
         a = at_s[pl.ds(j * 128, 128), :].T
         for n in range(3):
@@ -382,11 +433,10 @@
         return pltpu.make_async_copy(out_s.at[c], out.at[:, pl.ds(c * CW, CW)], osem)
 
     def combine(c):
-        recv_half = recv.at[c, pl.ds(0, 3 * bound), pl.ds(0, HW)]
-        await_bytes(recv_half, zfrecv.at[c])
-        z = recv[c]
+        await_bytes(recv.at[c, 0, pl.ds(0, 3 * bound), :], zfrecv.at[c])
+        z = jnp.concatenate([recv[c, 0], recv[c, 1]], axis=1)
         y = dot(a_s[2], z) + dot(a_s[1], z) + dot(a_s[0], z)
-        out_s[c] = (xr[c, pl.ds(k * TOK, TOK), :].astype(F32) + y).astype(BF16)
+        out_s[c] = (xo[c, pl.ds(k * TOK, TOK), :].astype(F32) + y).astype(BF16)
         out_copy(c).start()
 
     def step(c, _):
@@ -401,41 +451,46 @@
     await_bytes(seven, csend)
     await_bytes(seven, ksend)
     await_bytes(out_s, psend)
-    await_bytes(xs, xsend)
-    await_bytes(xs, xfsend)
+    for s in range(nz):
+        await_bytes(xs.at[s], xsend.at[s])
+    await_bytes(xl.at[:, 0], xfsend)
     forward(4)
     lax.fori_loop(0, NC, step, 0)
+    log_swap.wait_send()
+    for s in range(nq):
+        await_bytes(xin.at[s], xqsend.at[s])
     for s in range(2):
         await_bytes(q_bytes(s), qsend.at[s])
     for s in range(nz):
         await_bytes(zs.at[s], zsend.at[s])
-    await_bytes(recv.at[:, pl.ds(0, 3 * bound), pl.ds(0, HW)], zfsend)
+    await_bytes(recv.at[:, 0, pl.ds(0, 3 * bound), :], zfsend)
     await_bytes(out_s, osem)
 
 
-def moe_call(xb, bound, ge, ns1, ns2, nz, cid, tok, logit, w1, w2):
-    nx = -(-(2 * TOK + 6 * xb) // 128) * 128
+def moe_call(xb, bound, ge, ns1, ns2, nz, lag, cid, tok, logit, w1, w2):
+    nx = 2 * TOK + 3 * xb
     rows_in = -(-4 * bound // 128) * 128
     vm = pltpu.VMEM
     sem = pltpu.SemaphoreType.DMA
     sq = vm((ALL_EXP, TOK), F32)
     return pl.pallas_call(
-        functools.partial(moe_kernel, xb, nx, bound, ge, ns1, ns2, nz),
+        functools.partial(moe_kernel, xb, nx, bound, ge, ns1, ns2, nz, lag),
         out_shape=(jax.ShapeDtypeStruct((TOK, D), BF16), jax.ShapeDtypeStruct((1, 1), jnp.int32)),
         in_specs=[pl.BlockSpec(memory_space=pl.ANY)] * 4,
         out_specs=(pl.BlockSpec(memory_space=pl.ANY), pl.BlockSpec(memory_space=pltpu.SMEM)),
         scratch_shapes=[
-            vm((NC, nx, CW), BF16), vm((NC, 3 * xb, CW), BF16),
+            vm((NC, 2 * TOK, CW), BF16), vm((NC, 2, 3 * xb, HW), BF16), vm((2 * lag, 2, 3 * xb, HW), BF16),
+            vm((2 * lag, 3 * xb, HW), BF16), vm((nz, 3 * xb, HW), BF16), sq,
             vm((ns1, ge, CW, FF), BF16), vm((ns2, ge, FF, CW), BF16),
             sq, vm((8, ALL_EXP), F32), vm((64, ALL_EXP), F32), vm((8, ALL_EXP), F32), vm((64, ALL_EXP), F32),
             vm((16, TOK), F32), vm((3 * xb, TOK), BF16), sq,
             vm((SLOTS, nx), BF16), vm((SLOTS, 128), F32), vm((8, SLOTS), F32), vm((4 * bound, SLOTS), BF16),
-            vm((SLOTS, CW), BF16), vm((SLOTS, FF), F32), vm((SLOTS, FF), BF16), vm((SLOTS, CW), BF16),
-            vm((2, 4 * bound, CW), BF16), vm((2, 3 * bound, HW), BF16), vm((2, bound, CW), BF16),
-            vm((nz, 3 * bound, HW), BF16), vm((NC, rows_in, CW), BF16),
+            vm((SLOTS, CW), BF16), vm((nz, SLOTS, CW), BF16), vm((SLOTS, FF), F32), vm((SLOTS, FF), BF16), vm((SLOTS, CW), BF16),
+            vm((2, 2, 4 * bound, HW), BF16), vm((2, 4 * bound, HW), BF16), vm((2, bound, HW), BF16),
+            vm((nz, 3 * bound, HW), BF16), vm((NC, 2, rows_in, HW), BF16),
             sq, sq, vm((rows_in, TOK), F32), vm((3, TOK, rows_in), BF16), vm((NC, TOK, CW), BF16),
-            sem((ns1,)), sem((ns2,)), *[sem] * 11, sem((NC,)), sem((NC,)),
-            sem((nz,)), sem, sem((NC,)), sem((NC,)), sem((2,)), sem((2,)),
+            sem((ns1,)), sem((ns2,)), *[sem] * 7, sem((nz,)), *[sem] * 3, sem((NC,)), sem((NC,)),
+            sem((nz,)), sem, sem((NC,)), sem((NC,)), sem((2,)), sem((2,)), sem((2 * lag,)), sem((2 * lag,)), sem, sem,
         ],
         compiler_params=pltpu.CompilerParams(collective_id=cid, has_side_effects=True, vmem_limit_bytes=67043328),
         name=f"moe_{bound}",
@@ -447,8 +502,8 @@
     expert_spec = P("ep", None, None)
 
     def device_step(tok, logit, w1, w2):
-        out, flag = moe_call(144, 336, 8, 8, 8, NC, 0, tok, logit, w1, w2)
-        return lax.switch(flag[0, 0], (lambda: out, lambda: moe_call(TOK, 1024, 2, 2, 2, 2, 1, tok, logit, w1, w2)[0]))
+        out, flag = moe_call(256, 336, 8, 7, 7, NC, 2, 0, tok, logit, w1, w2)
+        return lax.switch(flag[0, 0], (lambda: out, lambda: moe_call(2 * TOK, 1024, 1, 2, 2, 1, 1, 1, tok, logit, w1, w2)[0]))
 
     return jax.shard_map(device_step, mesh=mesh, in_specs=(row_spec, row_spec, expert_spec, expert_spec),
                          out_specs=row_spec, check_vma=False)

time: 81.9 us -> 80.5 us (0.983)
  Pallas kernels: 78.6 us -> 77.2 us
    pallas_call x1, Pallas kernels: 78.6 us -> 77.2 us  [moe_call(): pl.pallas_call(functools.partial(moe_kernel, xb, nx, bound, ge, ns1, ns2,...]
where the time goes in v8:
time: 80.5 us; the launch traced here: 80.3 us
  Pallas kernels  77.2 us (96%)
  local copies, waits for them, and re-layouts  2.3 us (3%)
    pallas_call x1, Pallas kernels, moe_call(): pl.pallas_call(functools.partial(moe_kernel, xb, nx, bound, ge, ns1, ns2,...  77.2 us
    unnamed x1, local copies, waits for them, and re-layouts  2.3 us

profile of v8, /device:TPU:0, one launch (start us, length us, event | category | flops | bytes accessed | tf_op | source)
XLA Modules:
  0.0 80.3 jit_solution(14399197123953842737)
XLA Ops:
  0.0 77.2 %moe_336.1 = (bf16[256,2048]{1,0:T(8,128)(2,1)}, s32[1,1]{1,0:T(1,128)}) custom-call(bf16[256,2048]{1,0:T(8,128)(2,1)} %tok.1, f32[256,256]{1,0:T(8,128)} %logit.1, bf16[32,2048,512]{2,1,0:T(8,128)(2,1)} %w1.1, bf16[32,512,2048]{2,1,0:T(8,128)(2,1)} %w2.1), custom_call_target="tpu_custom_call" | custom-call | tf_op jit(solution)/shard_map/moe_336/pallas_call | solution.py:476
  77.8 0.2 conditional.1
  78.0 2.3 %copy.10 = bf16[256,2048]{1,0:T(8,128)(2,1)} copy(bf16[256,2048]{1,0:T(8,128)(2,1)} %get-tuple-element.26) | data formatting | bytes 2097152

commit v9 on v8

--- a/solution.py
+++ b/solution.py
@@ -322,7 +322,7 @@
     lax.fori_loop(0, NC - 1, chunk, 0)
     first_product(NC - 1, True)
 
-    RB = 64 if bound % 64 == 0 else 48
+    RB = 64 if bound % 64 == 0 else 88
 
     def build_a(n, _):
         o = n // (bound // RB)
@@ -502,7 +502,7 @@
     expert_spec = P("ep", None, None)
 
     def device_step(tok, logit, w1, w2):
-        out, flag = moe_call(256, 336, 8, 7, 7, NC, 2, 0, tok, logit, w1, w2)
+        out, flag = moe_call(256, 352, 8, 7, 7, NC, 2, 0, tok, logit, w1, w2)
         return lax.switch(flag[0, 0], (lambda: out, lambda: moe_call(2 * TOK, 1024, 1, 2, 2, 1, 1, 1, tok, logit, w1, w2)[0]))
 
     return jax.shard_map(device_step, mesh=mesh, in_specs=(row_spec, row_spec, expert_spec, expert_spec),

time: 80.5 us -> 81.8 us (1.016)
  Pallas kernels: 77.2 us -> 78.5 us
    pallas_call x1, Pallas kernels: 77.2 us -> 78.5 us  [moe_call(): pl.pallas_call(functools.partial(moe_kernel, xb, nx, bound, ge, ns1, ns2,...]
where the time goes in v9:
time: 81.8 us; the launch traced here: 81.6 us
  Pallas kernels  78.5 us (96%)
  local copies, waits for them, and re-layouts  2.3 us (3%)
    pallas_call x1, Pallas kernels, moe_call(): pl.pallas_call(functools.partial(moe_kernel, xb, nx, bound, ge, ns1, ns2,...  78.5 us
    unnamed x1, local copies, waits for them, and re-layouts  2.3 us

profile of v9, /device:TPU:0, one launch (start us, length us, event | category | flops | bytes accessed | tf_op | source)
XLA Modules:
  0.0 81.6 jit_solution(3234229105609235944)
XLA Ops:
  0.0 78.5 %moe_352.1 = (bf16[256,2048]{1,0:T(8,128)(2,1)}, s32[1,1]{1,0:T(1,128)}) custom-call(bf16[256,2048]{1,0:T(8,128)(2,1)} %tok.1, f32[256,256]{1,0:T(8,128)} %logit.1, bf16[32,2048,512]{2,1,0:T(8,128)(2,1)} %w1.1, bf16[32,512,2048]{2,1,0:T(8,128)(2,1)} %w2.1), custom_call_target="tpu_custom_call" | custom-call | tf_op jit(solution)/shard_map/moe_352/pallas_call | solution.py:476
  79.1 0.2 conditional.1
  79.3 2.3 %copy.10 = bf16[256,2048]{1,0:T(8,128)(2,1)} copy(bf16[256,2048]{1,0:T(8,128)(2,1)} %get-tuple-element.26) | data formatting | bytes 2097152
